TPU v7x, 128 devices: a whole 4x4x4 slice. The times are simulated.
128 devices in a mesh: row: 64 (over z, y, x), dp: 2 (over core).
Axes of the slice: x: 4, y: 4, z: 4, core: 2. Of those that a mesh axis runs over, the one named last changes fastest.
Arguments:
- x_tok: bfloat16 [131072, 256], P(('dp', 'row'))
- w_up: bfloat16 [256, 1024], replicated
- w_down: bfloat16 [1024, 128], replicated
- item_table: bfloat16 [1048576, 128], P('row')
- cand_ids: int32 [8192], replicated
- log_q: float32 [8192], replicated
- targets: int32 [131072], P(('dp', 'row'))
Outputs:
- output 1: float32 [], replicated
- output 2: float32 [1048576, 128], P('row')
- output 3: float32 [256, 1024], replicated
- output 4: float32 [1024, 128], replicated
All inputs are finite; a program needn't handle non-finite values.
Results may differ from a plain program's by a relative error of at most 0.002604.
Values are sent between devices in bfloat16 or wider.
A program may use at most 1 GiB of HBM per device.

v0:
```python
import functools

import jax
import jax.numpy as jnp
from jax import lax
from jax.experimental import pallas as pl
from jax.experimental.pallas import tpu as pltpu
from jax.sharding import PartitionSpec as P

ALL_AXES = ("dp", "row")
MESH = pl.DeviceIdType.MESH
CAP = 96
BLK = 512
TOK = 256
LANES = 128
ANY = pl.BlockSpec(memory_space=pl.ANY)
VMEM = pl.BlockSpec(memory_space=pltpu.VMEM)
SMEM = pl.BlockSpec(memory_space=pltpu.SMEM)


def params():
    return pltpu.CompilerParams(has_side_effects=True, vmem_limit_bytes=60 * 1024 * 1024)


def exchange(n_row, n_dp, both, *xs):
    n_x = len(xs)
    steps = range(n_dp) if both else range(1)
    n_out = n_row * (n_dp if both else 1)

    def kernel(*refs):
        ins, outs = refs[:n_x], refs[n_x:2 * n_x]
        send_sem, recv_sem = refs[2 * n_x:]
        row, dp = lax.axis_index("row"), lax.axis_index("dp")
        slot = dp * n_row + row if both else row
        for i in range(n_x):
            pltpu.make_async_copy(ins[i].at[row], outs[i].at[slot], recv_sem.at[i]).start()

        for e in steps:
            def send(j, carry, e=e):
                peer = lax.rem(row + j, n_row)
                for i in range(n_x):
                    pltpu.make_async_remote_copy(
                        src_ref=ins[i].at[peer],
                        dst_ref=outs[i].at[slot],
                        send_sem=send_sem.at[i, e],
                        recv_sem=recv_sem.at[i],
                        device_id={"row": peer, "dp": lax.rem(dp + e, n_dp)},
                        device_id_type=MESH,
                    ).start()
                return carry
            lax.fori_loop(0 if e else 1, n_row, send, 0)
        for i in range(n_x):
            for e in steps:
                sent = ins[i] if e else ins[i].at[pl.ds(0, n_row - 1)]
                pltpu.make_async_copy(sent, sent, send_sem.at[i, e]).wait()
            pltpu.make_async_copy(outs[i], outs[i], recv_sem.at[i]).wait()

    return pl.pallas_call(
        kernel,
        out_shape=[jax.ShapeDtypeStruct((n_out,) + x.shape[1:], x.dtype) for x in xs],
        in_specs=[VMEM] * n_x,
        out_specs=[VMEM] * n_x,
        scratch_shapes=[pltpu.SemaphoreType.DMA((n_x, n_dp)), pltpu.SemaphoreType.DMA((n_x,))],
        compiler_params=params(),
    )(*xs)


def pack(slot_row, vals, n_row):
    n_pad = slot_row.shape[1]
    per = 4 if n_row % 4 == 0 else 1

    def kernel(slot_ref, vals_ref, hid_ref, want_ref):
        base = pl.program_id(0) * (per * LANES)
        at = lax.broadcasted_iota(jnp.int32, (per * LANES, n_pad), 0) + base
        hit = (at == slot_ref[...]).astype(jnp.float32).astype(jnp.bfloat16)
        got = jnp.dot(hit, vals_ref[...], preferred_element_type=jnp.float32)
        for o in range(per):
            blk = got[o * LANES:(o + 1) * LANES]
            hid_ref[o] = blk[:CAP, :LANES].astype(jnp.bfloat16)
            ids = jnp.transpose(blk[:, LANES:])
            want_ref[o] = (ids[0:1] * 128.0 + ids[1:2]).astype(jnp.int32)

    return pl.pallas_call(
        kernel,
        grid=(n_row // per,),
        out_shape=[
            jax.ShapeDtypeStruct((n_row, CAP, LANES), jnp.bfloat16),
            jax.ShapeDtypeStruct((n_row, 1, LANES), jnp.int32),
        ],
        in_specs=[pl.BlockSpec((1, n_pad), lambda i: (0, 0)), pl.BlockSpec((n_pad, 2 * LANES), lambda i: (0, 0))],
        out_specs=[
            pl.BlockSpec((per, CAP, LANES), lambda i: (i, 0, 0)),
            pl.BlockSpec((per, 1, LANES), lambda i: (i, 0, 0)),
        ],
        compiler_params=pltpu.CompilerParams(vmem_limit_bytes=40 * 1024 * 1024),
    )(slot_row, vals)


def fetch(n_row, n_dp, want, table):
    rows_local, width = table.shape
    cut = min(1024, rows_local // 2)
    n_cut = rows_local // cut

    def kernel(want_ref, tab_ref, rows_ref, most_ref, tab16, tab32, asked, ask_s, stage, out_buf, sems, tab_sem):
        row, dp = lax.axis_index("row"), lax.axis_index("dp")

        def load(k, p):
            sl = pl.ds(pl.multiple_of(k * cut, cut), cut)
            return pltpu.make_async_copy(tab_ref.at[sl], tab16.at[p], tab_sem.at[p])
        load(0, 0).start()
        load(1, 1).start()
        pltpu.make_async_copy(want_ref.at[row], asked.at[row], sems.at[1]).start()

        def ask(j, carry):
            peer = lax.rem(row + j, n_row)
            pltpu.make_async_remote_copy(
                src_ref=want_ref.at[peer], dst_ref=asked.at[row], send_sem=sems.at[0], recv_sem=sems.at[1],
                device_id={"row": peer, "dp": dp}, device_id_type=MESH).start()
            return carry
        lax.fori_loop(1, n_row, ask, 0)

        def widen(k, more):
            for p in range(2):
                load(2 * k + p, p).wait()
                sl = pl.ds(pl.multiple_of((2 * k + p) * cut, cut), cut)
                tab32[sl, :] = tab16[p].astype(jnp.float32)
                if more:
                    load(2 * k + p + 2, p).start()
            return 0
        lax.fori_loop(0, n_cut // 2 - 1, lambda k, c: widen(k, True), 0)
        widen(n_cut // 2 - 1, False)
        pltpu.make_async_copy(asked, asked, sems.at[1]).wait()
        to_s = pltpu.make_async_copy(asked, ask_s, tab_sem.at[0])
        to_s.start()
        most_ref[...] = jnp.broadcast_to(jnp.max(asked[...], axis=0), (8, LANES))
        to_s.wait()

        def send(peer):
            pltpu.make_async_remote_copy(
                src_ref=out_buf.at[peer], dst_ref=rows_ref.at[row], send_sem=sems.at[2], recv_sem=sems.at[3],
                device_id={"row": peer, "dp": dp}, device_id_type=MESH).start()

        def gather(j):
            peer = lax.rem(row + j, n_row)
            for c in range(CAP):
                stage[pl.ds(c, 1), :] = tab32[pl.ds(ask_s[peer, 0, c], 1), :]
            out_buf[peer] = stage[...].astype(jnp.bfloat16)

        gather(1)

        def step(j, carry):
            gather(j)
            send(lax.rem(row + j - 1, n_row))
            return carry
        lax.fori_loop(2, n_row, step, 0)
        gather(n_row)
        send(lax.rem(row + n_row - 1, n_row))
        pltpu.make_async_copy(out_buf.at[row], rows_ref.at[row], sems.at[3]).start()
        sent = want_ref.at[pl.ds(0, n_row - 1)]
        pltpu.make_async_copy(sent, sent, sems.at[0]).wait()
        sent = out_buf.at[pl.ds(0, n_row - 1)]
        pltpu.make_async_copy(sent, sent, sems.at[2]).wait()
        pltpu.make_async_copy(rows_ref, rows_ref, sems.at[3]).wait()

    return pl.pallas_call(
        kernel,
        out_shape=[
            jax.ShapeDtypeStruct((n_row, CAP, width), table.dtype),
            jax.ShapeDtypeStruct((8, LANES), jnp.int32),
        ],
        in_specs=[VMEM, ANY],
        out_specs=[VMEM, VMEM],
        scratch_shapes=[
            pltpu.VMEM((2, cut, width), table.dtype),
            pltpu.VMEM((rows_local, width), jnp.float32),
            pltpu.VMEM((n_row, 1, LANES), jnp.int32),
            pltpu.SMEM((n_row, 1, LANES), jnp.int32),
            pltpu.VMEM((CAP, width), jnp.float32),
            pltpu.VMEM((n_row, CAP, width), table.dtype),
            pltpu.SemaphoreType.DMA((4,)),
            pltpu.SemaphoreType.DMA((2,)),
        ],
        compiler_params=params(),
    )(want, table)


def gather_cands(n_row, n_dp, my_cands, most):
    chunk, width = my_cands.shape

    def kernel(mine_ref, most_ref, all_ref, top_ref, theirs, sems):
        row, dp = lax.axis_index("row"), lax.axis_index("dp")
        other = lax.rem(dp + 1, n_dp)
        me = dp * n_row + row

        def one(j, carry):
            peer = lax.rem(row + j, n_row)
            pltpu.make_async_remote_copy(
                src_ref=mine_ref, dst_ref=all_ref.at[me], send_sem=sems.at[0], recv_sem=sems.at[1],
                device_id={"row": peer, "dp": dp}, device_id_type=MESH).start()
            return carry
        lax.fori_loop(1, n_row, one, 0)
        pltpu.make_async_copy(mine_ref, all_ref.at[me], sems.at[1]).start()
        count = pltpu.make_async_remote_copy(
            src_ref=most_ref, dst_ref=theirs, send_sem=sems.at[4], recv_sem=sems.at[5],
            device_id={"row": row, "dp": other}, device_id_type=MESH)
        count.start()
        half = all_ref.at[pl.ds(dp * n_row, n_row)]
        pltpu.make_async_copy(half, half, sems.at[1]).wait()
        swap = pltpu.make_async_remote_copy(
            src_ref=half, dst_ref=half, send_sem=sems.at[2], recv_sem=sems.at[3],
            device_id={"row": row, "dp": other}, device_id_type=MESH)
        swap.start()
        count.wait()
        top_ref[...] = jnp.maximum(most_ref[...], theirs[...])
        sent = all_ref.at[pl.ds(0, n_row - 1)]
        pltpu.make_async_copy(sent, sent, sems.at[0]).wait()
        swap.wait()

    return pl.pallas_call(
        kernel,
        out_shape=[
            jax.ShapeDtypeStruct((n_dp * n_row, chunk, width), my_cands.dtype),
            jax.ShapeDtypeStruct(most.shape, most.dtype),
        ],
        in_specs=[VMEM, VMEM],
        out_specs=[VMEM, VMEM],
        scratch_shapes=[pltpu.VMEM(most.shape, most.dtype), pltpu.SemaphoreType.DMA((6,))],
        compiler_params=params(),
    )(my_cands, most)


def softmax(n_total, cand_rows, hidden, tgt, y_lanes, cand_ids, log_q):
    n_cand, width = cand_rows.shape
    n_tok = hidden.shape[0]
    n_blk, n_sub = n_cand // BLK, n_tok // TOK
    f32 = jnp.float32

    def kernel(cands, h_ref, t_ref, y_ref, id_ref, lq_ref, cg_ref, dh_ref, dz_ref, loss_ref, z, g, h_t, acc, stat):
        h_t[...] = jnp.transpose(h_ref[...].astype(f32)).astype(jnp.bfloat16)
        for s in range(n_sub):
            tok = pl.ds(s * TOK, TOK)
            prod = h_ref[tok, :].astype(f32) * t_ref[tok, :].astype(f32)
            z_tgt = jnp.broadcast_to(jnp.sum(prod, axis=1, keepdims=True), (TOK, LANES))
            stat[0, tok, :] = z_tgt
            stat[1, tok, :] = z_tgt
        def logits(b, carry):
            rows = cands[pl.ds(pl.multiple_of(b * BLK, BLK), BLK), :]
            cols = pl.ds(pl.multiple_of(b * BLK, BLK), BLK)
            lq, cid = lq_ref[:, cols], id_ref[:, cols]

            def sub(s, c2):
                tok = pl.ds(pl.multiple_of(s * TOK, TOK), TOK)
                zz = lax.dot_general(h_ref[tok, :], rows, (((1,), (1,)), ((), ())), preferred_element_type=f32) - lq
                y = y_ref[tok, :]
                top = stat[1, tok, :]
                for k in range(BLK // LANES):
                    ln = slice(k * LANES, (k + 1) * LANES)
                    part = jnp.where(y == cid[:, ln], -1e9, zz[:, ln])
                    z[tok, pl.ds(pl.multiple_of(b * BLK + k * LANES, LANES), LANES)] = part
                    top = jnp.maximum(top, part)
                stat[1, tok, :] = top
                return c2
            return lax.fori_loop(0, n_sub, sub, carry)
        lax.fori_loop(0, n_blk, logits, 0)

        for s in range(n_sub):
            tok = pl.ds(s * TOK, TOK)
            stat[1, tok, :] = jnp.broadcast_to(jnp.max(stat[1, tok, :], axis=1, keepdims=True), (TOK, LANES))
            stat[2, tok, :] = jnp.zeros((TOK, LANES), f32)

        def exps(b, carry):
            def sub(s, c2):
                tok = pl.ds(pl.multiple_of(s * TOK, TOK), TOK)
                top = stat[1, tok, :]
                tot = stat[2, tok, :]
                for k in range(BLK // LANES):
                    at = pl.ds(pl.multiple_of(b * BLK + k * LANES, LANES), LANES)
                    e = jnp.exp(z[tok, at] - top)
                    z[tok, at] = e
                    tot = tot + e
                stat[2, tok, :] = tot
                return c2
            return lax.fori_loop(0, n_sub, sub, carry)
        lax.fori_loop(0, n_blk, exps, 0)

        loss_ref[...] = jnp.zeros_like(loss_ref)
        for s in range(n_sub):
            tok = pl.ds(s * TOK, TOK)
            z_tgt, top = stat[0, tok, :], stat[1, tok, :]
            e_tgt = jnp.exp(z_tgt - top)
            total = e_tgt + jnp.broadcast_to(jnp.sum(stat[2, tok, :], axis=1, keepdims=True), (TOK, LANES))
            dz = (e_tgt / total - 1.0) * (1.0 / n_total)
            dz_ref[tok, :] = dz
            stat[2, tok, :] = (1.0 / total) * (1.0 / n_total)
            part = top + jnp.log(total) - z_tgt
            loss_ref[...] += jnp.broadcast_to(jnp.sum(part, axis=0, keepdims=True), loss_ref.shape)
            acc[tok, :] = dz * t_ref[tok, :].astype(f32)

        def grads(b, carry):
            rows = cands[pl.ds(pl.multiple_of(b * BLK, BLK), BLK), :]

            def sub(s, c2):
                tok = pl.ds(pl.multiple_of(s * TOK, TOK), TOK)
                inv = stat[2, tok, :]
                for k in range(BLK // LANES):
                    at = pl.ds(pl.multiple_of(b * BLK + k * LANES, LANES), LANES)
                    g[tok, k * LANES:(k + 1) * LANES] = (z[tok, at] * inv).astype(jnp.bfloat16)
                acc[tok, :] += jnp.dot(g[tok, :], rows, preferred_element_type=f32)
                return c2
            lax.fori_loop(0, n_sub, sub, 0)
            cg_t = jnp.dot(h_t[...], g[...], preferred_element_type=f32)
            cg_ref[pl.ds(pl.multiple_of(b * BLK, BLK), BLK), :] = jnp.transpose(cg_t)
            return carry
        lax.fori_loop(0, n_blk, grads, 0)
        dh_ref[...] = acc[...].astype(jnp.bfloat16)

    return pl.pallas_call(
        kernel,
        out_shape=[
            jax.ShapeDtypeStruct((n_cand, width), f32),
            jax.ShapeDtypeStruct((n_tok, width), jnp.bfloat16),
            jax.ShapeDtypeStruct((n_tok, LANES), f32),
            jax.ShapeDtypeStruct((8, LANES), f32),
        ],
        in_specs=[VMEM] * 6,
        out_specs=[VMEM] * 4,
        scratch_shapes=[
            pltpu.VMEM((n_tok, n_cand), f32),
            pltpu.VMEM((n_tok, BLK), jnp.bfloat16),
            pltpu.VMEM((width, n_tok), jnp.bfloat16),
            pltpu.VMEM((n_tok, width), f32),
            pltpu.VMEM((3, n_tok, LANES), f32),
        ],
        compiler_params=pltpu.CompilerParams(vmem_limit_bytes=60 * 1024 * 1024),
    )(cand_rows, hidden, tgt, y_lanes, cand_ids, log_q)


def coords(row, side):
    return row // (side * side), lax.rem(row // side, side), lax.rem(row, side)


def order(part, z, y, x):
    return ((x, y, z), (y, z, x), (z, x, y))[part]


def row_of(part, a, b, c, side):
    z, y, x = ((c, b, a), (b, a, c), (a, c, b))[part]
    return (z * side + y) * side + x


def core_sum(side, cand, rest):
    n_row = side ** 3
    n_dp, rows = cand.shape[0], cand.shape[3]
    width = cand.shape[-1]

    def kernel(cand_ref, rest_ref, s0, s1, s2, cand_in, rest_in, sems):
        row, dp = lax.axis_index("row"), lax.axis_index("dp")
        other = lax.rem(dp + 1, n_dp)
        copies = [
            pltpu.make_async_remote_copy(
                src_ref=src.at[other], dst_ref=dst, send_sem=sems.at[i, 0], recv_sem=sems.at[i, 1],
                device_id={"row": row, "dp": other}, device_id_type=MESH)
            for i, (src, dst) in enumerate(((cand_ref, cand_in), (rest_ref, rest_in)))]
        for c in copies:
            c.start()
        for c in copies:
            c.wait()

        def one(r, carry):
            z, y, x = coords(r, side)
            a, b, c = order(0, z, y, x)
            s0[a, b, c] = cand_ref[dp, r, 0] + cand_in[r, 0]
            a, b, c = order(1, z, y, x)
            s1[a, b, c] = cand_ref[dp, r, 1] + cand_in[r, 1]
            a, b, c = order(2, z, y, x)
            s2[a, b, c] = rest_ref[dp, r] + rest_in[r]
            return carry
        lax.fori_loop(0, n_row, one, 0)

    lead = (side, side, side)
    return pl.pallas_call(
        kernel,
        out_shape=[jax.ShapeDtypeStruct(lead + (n, width), jnp.float32) for n in (rows, rows, rest.shape[2])],
        in_specs=[VMEM, VMEM],
        out_specs=[VMEM] * 3,
        scratch_shapes=[
            pltpu.VMEM(cand.shape[1:], jnp.float32),
            pltpu.VMEM(rest.shape[1:], jnp.float32),
            pltpu.SemaphoreType.DMA((2, 2)),
        ],
        compiler_params=params(),
    )(cand, rest)


def axis_sum(side, parts, moved):
    n_row = side ** 3
    n_p, n_m = len(parts), len(moved)
    f32 = jnp.float32

    def kernel(*refs):
        refs = list(refs)
        take = lambda n: [refs.pop(0) for _ in range(n)]
        s, out = take(n_p), take(n_m)
        g, into = take(n_p), take(n_m)
        r1, t1, r2, t2, r3 = (take(n_p) for _ in range(5))
        sems, m_sems = refs
        row, dp = lax.axis_index("row"), lax.axis_index("dp")
        z, y, x = coords(row, side)
        at = [order(p, z, y, x) for p in range(n_p)]

        def send(p, phase, axis, k, src, dst):
            to = list(at[p])
            to[axis] = lax.rem(to[axis] + k, side)
            pltpu.make_async_remote_copy(
                src_ref=src(to[axis]), dst_ref=dst, send_sem=sems.at[p, phase, 0], recv_sem=sems.at[p, phase, 1],
                device_id={"row": row_of(p, *to, side), "dp": dp}, device_id_type=MESH).start()

        def wait(p, phase, d, like):
            pltpu.make_async_copy(like, like, sems.at[p, phase, d]).wait()

        def move(lo, hi):
            def one(j, carry):
                peer = lax.rem(row + j, n_row)
                for i in range(n_m):
                    pltpu.make_async_remote_copy(
                        src_ref=out[i].at[peer], dst_ref=into[i].at[row], send_sem=m_sems.at[i, 0], recv_sem=m_sems.at[i, 1],
                        device_id={"row": peer, "dp": dp}, device_id_type=MESH).start()
                return carry
            lax.fori_loop(lo, hi, one, 0)
        cuts = [1 + (n_row - 1) * i // 6 for i in range(7)]

        src_of = (s, t1, t2)
        got_of = (r1, r2, r3)
        sum_of = (t1, t2, None)
        for phase in range(3):
            for p in range(n_p):
                for k in range(1, side):
                    send(p, phase, phase, k, lambda i, p=p: src_of[phase][p].at[i], got_of[phase][p].at[at[p][phase]])
            move(cuts[phase], cuts[phase + 1])
            if phase == 0:
                for i in range(n_m):
                    pltpu.make_async_copy(out[i].at[row], into[i].at[row], m_sems.at[i, 1]).start()
            for p in range(n_p):
                mine, got = src_of[phase][p], got_of[phase][p]
                wait(p, phase, 1, got.at[pl.ds(0, side - 1)])
                me = at[p][phase]

                def total(idx, p=p, mine=mine, got=got, me=me):
                    v = mine[(me,) + idx]
                    for k in range(1, side):
                        v = v + got[(lax.rem(me + k, side),) + idx]
                    return v
                if phase == 0:
                    def body(i, carry, p=p, total=total):
                        for j in range(side):
                            t1[p][i, j] = total((i, j))
                        return carry
                    lax.fori_loop(0, side, body, 0)
                elif phase == 1:
                    def body(i, carry, p=p, total=total):
                        t2[p][i] = total((i,))
                        return carry
                    lax.fori_loop(0, side, body, 0)
                else:
                    g[p][at[p][0], at[p][1], at[p][2]] = total(())

        for phase in range(3, 6):
            axis = 5 - phase
            for p in range(n_p):
                blk = g[p].at[at[p][:axis + 1]]
                for k in range(1, side):
                    send(p, phase, axis, k, lambda i, blk=blk: blk, blk)
            move(cuts[phase], cuts[phase + 1])
            for p in range(n_p):
                wait(p, phase, 1, g[p].at[at[p][:axis] + (pl.ds(0, side - 1),)])
        for p in range(n_p):
            for phase in range(3):
                wait(p, phase, 0, src_of[phase][p].at[pl.ds(0, side - 1)])
                axis = 2 - phase
                wait(p, phase + 3, 0, g[p].at[at[p][:axis] + (pl.ds(0, side - 1),)])
        for i in range(n_m):
            sent = out[i].at[pl.ds(0, n_row - 1)]
            pltpu.make_async_copy(sent, sent, m_sems.at[i, 0]).wait()
            pltpu.make_async_copy(into[i], into[i], m_sems.at[i, 1]).wait()

    same = [jax.ShapeDtypeStruct(v.shape, v.dtype) for v in list(parts) + list(moved)]
    scratch = [[pltpu.VMEM(shape(v.shape), f32) for v in parts] for shape in (
        lambda q: q, lambda q: q[1:], lambda q: q[1:], lambda q: q[2:], lambda q: q[2:])]
    return pl.pallas_call(
        kernel,
        out_shape=same,
        in_specs=[VMEM] * len(same),
        out_specs=[VMEM] * len(same),
        scratch_shapes=[v for group in scratch for v in group] + [
            pltpu.SemaphoreType.DMA((n_p, 6, 2)), pltpu.SemaphoreType.DMA((n_m, 2))],
        compiler_params=params(),
    )(*parts, *moved)


def core_swap(n_dp, *xs):
    n = len(xs)

    def kernel(*refs):
        ins, outs, sems = refs[:n], refs[n:2 * n], refs[2 * n]
        row, dp = lax.axis_index("row"), lax.axis_index("dp")
        other = lax.rem(dp + 1, n_dp)
        copies = []
        for i in range(n):
            copies.append(pltpu.make_async_remote_copy(
                src_ref=ins[i], dst_ref=outs[i].at[dp], send_sem=sems.at[i, 0], recv_sem=sems.at[i, 1],
                device_id={"row": row, "dp": other}, device_id_type=MESH))
            copies.append(pltpu.make_async_copy(ins[i], outs[i].at[dp], sems.at[i, 2]))
        for c in copies:
            c.start()
        for c in copies:
            c.wait()

    return pl.pallas_call(
        kernel,
        out_shape=[jax.ShapeDtypeStruct((n_dp,) + x.shape, x.dtype) for x in xs],
        in_specs=[VMEM] * n,
        out_specs=[VMEM] * n,
        scratch_shapes=[pltpu.SemaphoreType.DMA((n, 3))],
        compiler_params=params(),
    )(*xs)


def add_rows(n_rows, groups, grad=None, n_acc=4):
    width = groups[0][2].shape[1]
    n_full = n_rows + 8
    chunk = min(128, n_rows)
    flat, specs = [], []
    for row_ids, counts, vals, val_ids in groups:
        flat += [row_ids, counts, vals] + ([] if val_ids is None else [val_ids])
        specs += [SMEM, SMEM, VMEM] + ([] if val_ids is None else [SMEM])
    if grad is not None:
        flat.append(grad)
        specs.append(ANY)

    def kernel(*refs):
        refs = list(refs)
        work = []
        for _, _, vals, val_ids in groups:
            idx, cnt, ref = refs.pop(0), refs.pop(0), refs.pop(0)
            work.append((idx, cnt, ref, None if val_ids is None else refs.pop(0)))
        grad_ref = refs.pop(0) if grad is not None else None
        out_ref, sem = refs[0], refs[-1]
        accs = refs[1:-1]
        if grad_ref is not None:
            cp_in = pltpu.make_async_copy(grad_ref, accs[0].at[pl.ds(0, n_rows)], sem)
            cp_in.start()
        fresh = accs if grad_ref is None else accs[1:]

        def clear(k, carry):
            for a in fresh:
                a[pl.ds(pl.multiple_of(k * chunk, chunk), chunk), :] = jnp.zeros((chunk, width), jnp.float32)
            return carry
        if fresh:
            lax.fori_loop(0, n_rows // chunk, clear, 0)
        for a in accs:
            a[pl.ds(n_rows, 8), :] = jnp.zeros((8, width), jnp.float32)
        if grad_ref is not None:
            cp_in.wait()

        for idx, cnt, vals_ref, vid in work:
            per_list = vals_ref.shape[0] // idx.shape[0]

            def one_list(i, carry, idx=idx, cnt=cnt, vals_ref=vals_ref, vid=vid, per_list=per_list):
                def group(q, c2):
                    for u in range(8):
                        c = q * 8 + u
                        acc = accs[u % n_acc]
                        r = idx[i, c]
                        v = i * per_list + c if vid is None else vid[i, c]
                        acc[pl.ds(r, 1), :] += vals_ref[pl.ds(v, 1), :]
                    return c2
                return lax.fori_loop(0, (cnt[i] + 7) // 8, group, carry)
            lax.fori_loop(0, idx.shape[0], one_list, 0)

        if n_acc > 1:
            def merge(k, carry):
                sl = pl.ds(pl.multiple_of(k * chunk, chunk), chunk)
                tot = accs[0][sl, :]
                for a in accs[1:]:
                    tot = tot + a[sl, :]
                accs[0][sl, :] = tot
                return carry
            lax.fori_loop(0, n_rows // chunk, merge, 0)
        cp_out = pltpu.make_async_copy(accs[0].at[pl.ds(0, n_rows)], out_ref, sem)
        cp_out.start()
        cp_out.wait()

    return pl.pallas_call(
        kernel,
        out_shape=jax.ShapeDtypeStruct((n_rows, width), jnp.float32),
        in_specs=specs,
        out_specs=ANY,
        scratch_shapes=[pltpu.VMEM((n_full, width), jnp.float32)] * n_acc + [pltpu.SemaphoreType.DMA],
        compiler_params=pltpu.CompilerParams(vmem_limit_bytes=60 * 1024 * 1024),
    )(*flat)


def ranks(owner, n_row):
    n = owner.shape[0]
    hot = (owner[:, None] == jnp.arange(n_row)[None, :]).astype(jnp.bfloat16)
    pos = jnp.arange(n)
    before = (pos[:, None] > pos[None, :]).astype(jnp.bfloat16)
    earlier = jnp.dot(before, hot, preferred_element_type=jnp.float32)
    hot32 = hot.astype(jnp.float32)
    return jnp.sum(earlier * hot32, axis=1).astype(jnp.int32), jnp.sum(hot32, axis=0).astype(jnp.int32)


def to_slots(slot, vals, n_slots):
    hit = slot[:, None] == jnp.arange(n_slots)[None, :]
    return [jnp.sum(jnp.where(hit, v[:, None], jnp.zeros((), v.dtype)), axis=0) for v in vals]


def tile_rows(rows, n_row):
    padded = [jnp.pad(r, ((0, 0), (0, LANES - r.shape[1]))) for r in rows]
    padded += [jnp.zeros_like(padded[0])] * (8 - len(rows))
    return jnp.stack(padded, axis=1)


def solution(mesh):
    n_row, n_dp = mesh.shape["row"], mesh.shape["dp"]
    n_dev = n_row * n_dp
    side = round(n_row ** (1 / 3))

    def run_step(x_tok, w_up, w_down, item_table, cand_ids, log_q, targets):
        n_total = x_tok.shape[0]

        def device_step(x_loc, w_up, w_down, tab_loc, cand_ids, log_q, y_loc):
            rows_local, width = tab_loc.shape
            n_tok = y_loc.shape[0]
            n_cand = cand_ids.shape[0]
            row, dp = lax.axis_index("row"), lax.axis_index("dp")
            me = dp * n_row + row
            chunk = n_cand // n_dev
            f32, bf16 = jnp.float32, jnp.bfloat16
            n_ids = n_tok + chunk
            n_pad = -(-n_ids // LANES) * LANES

            my_cands = lax.dynamic_slice_in_dim(cand_ids, me * chunk, chunk)
            ids = jnp.concatenate([y_loc, my_cands])
            owner, local = ids // rows_local, ids % rows_local
            rank, per_owner = ranks(owner, n_row)
            most = jnp.max(per_owner)

            pre_act = jnp.dot(x_loc, w_up, preferred_element_type=f32)
            act_full, gelu_vjp = jax.vjp(jax.nn.gelu, pre_act)
            act_b = act_full.astype(bf16)
            hidden = jnp.dot(act_b, w_down, preferred_element_type=f32).astype(bf16)

            split = jnp.pad(jnp.stack([local // 128, local % 128], axis=1).astype(bf16), ((0, n_pad - n_ids), (0, LANES - 2)))
            carried = jnp.concatenate([jnp.pad(hidden, ((0, n_pad - n_tok), (0, 0))), split], axis=1)

            def pack_round(k):
                rel = rank - k * CAP
                hit = (rel >= 0) & (rel < CAP)
                slot = jnp.where(hit, owner * LANES + rel, -1)
                hid_out, want = pack(jnp.pad(slot, (0, n_pad - n_ids), constant_values=-1)[None, :], carried, n_row)
                return hit, owner * CAP + rel, hid_out, want

            def fetch_round(k):
                hit, at, hid_out, want = pack_round(k)
                lane = jnp.arange(LANES)[None, None, :]
                rows_in, most_all = fetch(n_row, n_dp, jnp.where(lane == LANES - 1, most, want), tab_loc)
                got = jnp.take(rows_in.reshape(n_row * CAP, width), at, axis=0, mode="clip")
                return hit, got, hid_out, most_all

            _, got, hid_out, most_dp = fetch_round(0)
            cand_rows, most_all = gather_cands(n_row, n_dp, got[n_tok:], most_dp)
            most_all = most_all[0, LANES - 1]

            def fetch_more(carry):
                k, got, _ = carry
                hit, new, _, most = fetch_round(k)
                got = jnp.where(hit[:, None], new, got)
                return k + 1, got, gather_cands(n_row, n_dp, got[n_tok:], most)[0]

            _, got, cand_rows = lax.while_loop(
                lambda c: c[0] * CAP < most_all, fetch_more, (jnp.int32(1), got, cand_rows))
            tgt_rows, cand_rows = got[:n_tok], cand_rows.reshape(n_cand, width)

            cand_grad, grad_hid, dz_lanes, loss_part = softmax(
                n_total, cand_rows, hidden, tgt_rows,
                jnp.broadcast_to(y_loc[:, None], (n_tok, LANES)), cand_ids[None, :], log_q[None, :])
            dz_tgt, loss_sum = dz_lanes[:, 0], loss_part[0, 0]

            grad_down = jnp.einsum("tf,td->fd", act_b, grad_hid, preferred_element_type=f32)
            grad_act = jnp.einsum("td,fd->tf", grad_hid, w_down, preferred_element_type=f32)
            grad_pre = gelu_vjp(grad_act)[0].astype(bf16)
            grad_up = jnp.einsum("ti,tf->if", x_loc, grad_pre, preferred_element_type=f32)

            t_rank, t_owner, t_local = rank[:n_tok], owner[:n_tok], local[:n_tok]
            t_count = jnp.sum((t_owner[:, None] == jnp.arange(n_row)[None, :]).astype(jnp.int32), axis=0)
            c_rank, _ = ranks(owner[n_tok:], n_row)
            c_slot = owner[n_tok:] * chunk + c_rank
            c_count = per_owner - t_count
            c_row, c_pos = to_slots(c_slot, [(local[n_tok:] - rows_local).astype(f32), jnp.arange(chunk, dtype=f32)], n_row * chunk)
            c_row = (c_row + rows_local).reshape(n_row, chunk)
            c_pos = c_pos.reshape(n_row, chunk)
            half, z_y_x = chunk // 2, coords(row, side)
            first = []
            for part in range(2):
                a, b, c = order(part, *z_y_x)
                first.append((((part * n_dp + dp) * n_row + (a * side + b) * side + c) * half).astype(f32))
            c_pos = jnp.where(c_pos < half, first[0] + c_pos, first[1] + c_pos - half)

            def give(k):
                rel = t_rank - k * CAP
                slot = jnp.where((rel >= 0) & (rel < CAP), t_owner * CAP + rel, -1)
                t_row, t_dz = to_slots(slot, [t_local.astype(f32), dz_tgt], n_row * CAP)
                now = jnp.clip(t_count - k * CAP, 0, CAP).astype(f32)
                counts = jnp.stack([now, c_count.astype(f32), jnp.full((n_row,), loss_sum)], axis=1)
                return tile_rows([t_row.reshape(n_row, CAP), t_dz.reshape(n_row, CAP), c_row, c_pos, counts], n_row)

            to_int = lambda v: v.astype(jnp.int32)

            def token_group(hid_in, meta_in):
                vals = meta_in[:, 1, :CAP, None] * hid_in.astype(f32)
                return to_int(meta_in[:, 0, :CAP]), to_int(meta_in[:, 4, 0]), vals.reshape(n_dev * CAP, width), None

            blocks = w_up.shape[1] // LANES
            up_shape = (n_dev // blocks, w_up.shape[0] * blocks // n_dev, blocks, LANES)
            rest = jnp.concatenate([
                grad_up.reshape(up_shape).transpose(0, 2, 1, 3).reshape(n_dp, n_row, up_shape[1], width),
                grad_down.reshape(n_dp, n_row, -1, width)], axis=2)
            parts = core_sum(side, cand_grad.reshape(n_dp, n_row, 2, half, width), rest)
            g0, g1, g2, hid_in, meta_in = axis_sum(side, parts, [hid_out, give(0)])
            g0, g1, g2, hid_in, meta_in = core_swap(n_dp, g0, g1, g2, hid_in, meta_in)
            hid_in, meta_in = hid_in.reshape(n_dev, CAP, width), meta_in.reshape(n_dev, 8, LANES)
            cand_sums = jnp.concatenate([g0.reshape(-1, width), g1.reshape(-1, width)], axis=0)
            rest = jnp.transpose(g2, (0, 1, 3, 2, 4, 5)).reshape(n_dev, -1, width)
            grad_up = rest[:, :up_shape[1]].reshape(up_shape[0], blocks, up_shape[1], LANES).transpose(0, 2, 1, 3).reshape(w_up.shape)
            grad_down = rest[:, up_shape[1]:].reshape(w_down.shape)

            grad = add_rows(rows_local, [
                token_group(hid_in, meta_in),
                (to_int(meta_in[:, 2, :chunk]), to_int(meta_in[:, 4, 1]), cand_sums, to_int(meta_in[:, 3, :chunk]))])

            def give_more(carry):
                k, grad = carry
                return k + 1, add_rows(rows_local, [token_group(*exchange(n_row, n_dp, True, pack_round(k)[2], give(k)))], grad, 1)

            _, grad = lax.while_loop(lambda c: c[0] * CAP < most_all, give_more, (jnp.int32(1), grad))
            return jnp.sum(meta_in[:, 4, 2]) / n_total, grad, grad_up, grad_down

        return jax.shard_map(
            device_step,
            mesh=mesh,
            in_specs=(P(ALL_AXES, None), P(), P(), P("row", None), P(), P(), P(ALL_AXES)),
            out_specs=(P(), P("row", None), P(), P()),
            check_vma=False,
        )(x_tok, w_up, w_down, item_table, cand_ids, log_q, targets)

    return run_step
```

profile of v0, /device:TPU:1, one launch (start us, length us, event | category | flops | bytes accessed | tf_op | source)
XLA Modules:
  0.0 402.0 jit_solution(6223436136357980538)
XLA Ops:
  5.2 1.2 convert_bitcast_fusion.2
  8.9 0.9 copy.51
  9.8 1.7 broadcast_in_dim.184.y_ref
  11.5 4.5 %multiply_convert_fusion = (bf16[1024,1024]{1,0:T(8,128)(2,1)S(1)}, f32[1024,1024]{1,0:T(8,128)}) fusion(bf16[1024,256]{1,0:T(8,128)(2,1)S(1)} %copy-done, bf16[256,1024]{1,0:T(8,128)(2,1)} %param.12), kind=kOutput, calls=%fused_computation.36 | convolution fusion | flops 546308096 | bytes 7340032 | tf_op jit(solution)/shard_map/dot_general | solution.py:649
  16.9 8.8 %shard_map.102 = (bf16[64,96,128]{2,1,0:T(8,128)(2,1)S(1)}, s32[64,1,128]{2,1,0:T(1,128)S(1)}) custom-call(s32[1,1152]{1,0:T(1,128)S(1)} %broadcast_in_dim.183.slot_ref, bf16[1152,256]{1,0:T(8,128)(2,1)S(1)} %fusion.16.vals_ref), custom_call_target="tpu_custom_call" | custom-call | tf_op jit(solution)/shard_map/pallas_call | solution.py:83
  25.7 1.2 copy-done.3
  26.9 1.3 broadcast_select_fusion.2.want_ref
  28.1 48.7 %shard_map.103 = (bf16[64,96,128]{2,1,0:T(8,128)(2,1)}, s32[8,128]{1,0:T(8,128)}) custom-call(s32[64,1,128]{2,1,0:T(1,128)} %broadcast_select_fusion.2.want_ref, bf16[16384,128]{1,0:T(8,128)(2,1)} %tab_ref.1), custom_call_target="tpu_custom_call" | custom-call | tf_op jit(solution)/shard_map/pallas_call | solution.py:165
  76.8 4.7 %gather_fusion.1 = bf16[1088,128]{1,0:T(8,128)(2,1)} fusion(bf16[6144,128]{1,0:T(8,128)(2,1)} %bitcast.126, s32[2048]{0:T(1024)S(1)} %pad_clamp_fusion.1), kind=kCustom, calls=%fused_computation.1 | custom fusion | bytes 561408 | tf_op jit(solution)/shard_map/jit(_take)/gather | solution.py:668
  81.6 1.3 slice.104.mine_ref
  82.9 30.6 %shard_map.104 = (bf16[128,64,128]{2,1,0:T(8,128)(2,1)}, s32[8,128]{1,0:T(8,128)}) custom-call(bf16[64,128]{1,0:T(8,128)(2,1)} %slice.104.mine_ref, s32[8,128]{1,0:T(8,128)} %get-tuple-element.273.most_ref), custom_call_target="tpu_custom_call" | custom-call | tf_op jit(solution)/shard_map/pallas_call | solution.py:219
  113.5 1.3 slice.80
  114.8 0.9 while.24
  115.7 1.7 slice.81.t_ref
  117.4 54.9 %shard_map.105 = (f32[8192,128]{1,0:T(8,128)}, bf16[1024,128]{1,0:T(8,128)(2,1)}, f32[1024,128]{1,0:T(8,128)}, f32[8,128]{1,0:T(8,128)}) custom-call(bf16[8192,128]{1,0:T(8,128)(2,1)} %bitcast.127, bf16[1024,128]{1,0:T(8,128)(2,1)} %copy-done.5, bf16[1024,128]{1,0:T(8,128)(2,1)} %slice.81.t_ref, s32[1024,128]{1,0:T(8,128)} %broadcast_in_dim.184.y_ref, ...), custom_call_target="tpu_custom_call" | custom-call | tf_op jit(solution)/shard_map/pallas_call | solution.py:317
  172.3 6.7 %fusion.11 = f32[256,1024]{0,1:T(8,128)} fusion(bf16[1024,256]{1,0:T(8,128)(2,1)S(1)} %copy-done, f32[1024,1024]{1,0:T(8,128)} %get-tuple-element.434, bf16[1024,128]{1,0:T(8,128)(2,1)} %get-tuple-element.279, bf16[1024,128]{1,0:T(8,128)(2,1)} %param.13), kind=kOutput, calls=%fused_computation.40 | convolution fusion | flops 826277888 | bytes 6291456 | tf_op jit(solution)/shard_map/ti,tf->if/dot_general | solution.py:693
  179.7 1.6 copy.52
  181.8 1.2 pad_maximum_fusion.1.rest_ref
  183.1 1.3 slice.88
  184.3 35.1 %shard_map.106 = (f32[4,4,4,32,128]{4,3,2,1,0:T(8,128)}, f32[4,4,4,32,128]{4,3,2,1,0:T(8,128)}, f32[4,4,4,24,128]{4,3,2,1,0:T(8,128)}) custom-call(f32[2,64,2,32,128]{4,3,2,1,0:T(8,128)} %bitcast.115, f32[2,64,24,128]{3,2,1,0:T(8,128)} %pad_maximum_fusion.1.rest_ref), custom_call_target="tpu_custom_call" | custom-call | tf_op jit(solution)/shard_map/pallas_call | solution.py:381
  220.7 9.4 %select_reduce_fusion.2 = (f32[6144]{0:T(1024)S(1)}, f32[6144]{0:T(1024)S(1)}) fusion(f32[1024]{0:T(1024)S(1)} %get-tuple-element.420, s32[1024]{0:T(1024)S(1)} %copy-done.19, f32[1024]{0:T(1024)S(1)} %copy-done.18), kind=kLoop, calls=%fused_computation.20 | loop fusion | flops 31444992 | bytes 61440 | tf_op jit(solution)/shard_map/reduce_sum | solution.py:615
  230.4 1.0 stack.77.refs_4_
  231.4 84.5 %shard_map.107 = (f32[4,4,4,32,128]{4,3,2,1,0:T(8,128)}, f32[4,4,4,32,128]{4,3,2,1,0:T(8,128)}, f32[4,4,4,24,128]{4,3,2,1,0:T(8,128)}, bf16[64,96,128]{2,1,0:T(8,128)(2,1)}, f32[64,8,128]{2,1,0:T(8,128)}) custom-call(f32[4,4,4,32,128]{4,3,2,1,0:T(8,128)} %get-tuple-element.280.refs_0_, f32[4,4,4,32,128]{4,3,2,1,0:T(8,128)} %get-tuple-element.281.refs_1_, ...), custom_call_target="tpu_custom_call" | custom-call | tf_op jit(solution)/shard_map/pallas_call | solution.py:489
  315.9 25.7 %shard_map.108 = (f32[2,4,4,4,32,128]{5,4,3,2,1,0:T(8,128)}, f32[2,4,4,4,32,128]{5,4,3,2,1,0:T(8,128)}, f32[2,4,4,4,24,128]{5,4,3,2,1,0:T(8,128)}, bf16[2,64,96,128]{3,2,1,0:T(8,128)(2,1)}, f32[2,64,8,128]{3,2,1,0:T(8,128)}) custom-call(f32[4,4,4,32,128]{4,3,2,1,0:T(8,128)} %get-tuple-element.286.refs_0_, f32[4,4,4,32,128]{4,3,2,1,0:T(8,128)} %get-tuple-element.287.refs_1_, ...), custom_call_target="tpu_custom_call" | custom-call | tf_op jit(solution)/shard_map/pallas_call | solution.py:518
  341.6 1.1 copy.55
  346.3 1.6 copy.57
  347.9 0.8 slice_bitcast_fusion
  349.2 1.2 copy.63
  350.3 3.8 convert_multiply_fusion.1.refs_2_
  354.3 2.3 pad_maximum_fusion.refs_5_
  356.6 42.4 %shard_map.109 = f32[16384,128]{1,0:T(8,128)} custom-call(s32[128,96]{1,0:T(8,128)} %get-tuple-element.424.refs_0_, s32[128]{0:T(128)} %get-tuple-element.360.refs_1_, f32[12288,128]{1,0:T(8,128)} %convert_multiply_fusion.1.refs_2_, s32[128,64]{1,0:T(8,128)} %get-tuple-element.422.refs_3_, s32[128]{0:T(128)} %get-tuple-element.359.refs_4_, ...), custom_call_target="tpu_custom_call" | custom-call | tf_op jit(solution)/shard_map/pallas_call | solution.py:593
  399.7 1.0 copy-done.1
  (97 shorter events, 14.5 us)
Async XLA Ops:
  0.6 10.9 %copy-start = (bf16[1024,256]{1,0:T(8,128)(2,1)S(1)}, bf16[1024,256]{1,0:T(8,128)(2,1)}, u32[]{:S(2)}) copy-start(bf16[1024,256]{1,0:T(8,128)(2,1)} %param.11) | copy-start | bytes 1572868
  5.2 1.2 copy-start.20
  7.7 8.4 %copy-start.8 = (f32[64,64]{1,0:T(8,128)}, f32[64,64]{1,0:T(8,128)S(1)}, u32[]{:S(2)}) copy-start(f32[64,64]{1,0:T(8,128)S(1)} %add.212) | copy-start | bytes 49156
  11.5 4.5 %copy-start.12 = (bf16[1024,128]{1,0:T(8,128)(2,1)S(1)}, bf16[1024,128]{1,0:T(8,128)(2,1)}, u32[]{:S(2)}) copy-start(bf16[1024,128]{1,0:T(8,128)(2,1)} %param.13) | copy-start | bytes 786436
  11.5 5.2 %copy-start.10 = (bf16[1088,2]{1,0:T(8,128)(2,1)S(1)}, bf16[1088,2]{1,0:T(8,128)(2,1)}, u32[]{:S(2)}) copy-start(bf16[1088,2]{1,0:T(8,128)(2,1)} %copy.51) | copy-start | bytes 13060
  16.0 10.8 %copy-start.23 = (pred[128]{0:T(512)(128)(4,1)S(1)}, pred[128]{0:T(512)(128)(4,1)}, u32[]{:S(2)}) copy-start(pred[128]{0:T(512)(128)(4,1)} %iota_compare_fusion.19) | copy-start | bytes 388
  16.8 64.8 %copy-start.5 = (bf16[1024,128]{1,0:T(8,128)(2,1)}, bf16[1024,128]{1,0:T(8,128)(2,1)S(1)}, u32[]{:S(2)}) copy-start(bf16[1024,128]{1,0:T(8,128)(2,1)S(1)} %convolution_convert_fusion.h_ref) | copy-start | bytes 786436
  25.7 1.2 copy-start.3
  172.3 6.7 %copy-start.13 = (bf16[1024,128]{1,0:T(8,128)(2,1)S(1)}, bf16[1024,128]{1,0:T(8,128)(2,1)}, u32[]{:S(2)}) copy-start(bf16[1024,128]{1,0:T(8,128)(2,1)} %get-tuple-element.279) | copy-start | bytes 786436
  181.8 38.4 %copy-start.17 = (f32[64,1]{0,1:T(1,128)S(1)}, f32[64,1]{0,1:T(1,128)}, u32[]{:S(2)}) copy-start(f32[64,1]{0,1:T(1,128)} %get-tuple-element.656) | copy-start | bytes 772
  181.8 38.4 %copy-start.22 = (f32[64,1]{0,1:T(1,128)S(1)}, f32[64,1]{0,1:T(1,128)}, u32[]{:S(2)}) copy-start(f32[64,1]{0,1:T(1,128)} %get-tuple-element.430) | copy-start | bytes 772
  181.8 38.6 %copy-start.11 = (f32[1024,128]{1,0:T(8,128)S(1)}, f32[1024,128]{1,0:T(8,128)}, u32[]{:S(2)}) copy-start(f32[1024,128]{1,0:T(8,128)} %get-tuple-element.284) | copy-start | bytes 1572868
  183.0 37.7 %copy-start.18 = (f32[1024]{0:T(1024)S(1)}, f32[1024]{0:T(1024)}, u32[]{:S(2)}) copy-start(f32[1024]{0:T(1024)} %get-tuple-element.435) | copy-start | bytes 12292
  183.0 37.7 %copy-start.19 = (s32[1024]{0:T(1024)S(1)}, s32[1024]{0:T(1024)}, u32[]{:S(2)}) copy-start(s32[1024]{0:T(1024)} %get-tuple-element.426) | copy-start | bytes 12292
  183.0 47.3 %copy-start.15 = (f32[64,128]{1,0:T(8,128)S(1)}, f32[64,128]{1,0:T(8,128)}, u32[]{:S(2)}) copy-start(f32[64,128]{1,0:T(8,128)} %pad.78) | copy-start | bytes 98308
  183.0 47.3 %copy-start.16 = (f32[64,128]{1,0:T(8,128)S(1)}, f32[64,128]{1,0:T(8,128)}, u32[]{:S(2)}) copy-start(f32[64,128]{1,0:T(8,128)} %pad.79) | copy-start | bytes 98308
  347.9 2.4 copy-start.4
  350.3 3.8 copy-start.6
  350.3 3.9 copy-start.7
  356.6 42.4 %copy-start.9 = (f32[64,64]{1,0:T(8,128)S(1)}, f32[64,64]{1,0:T(8,128)}, u32[]{:S(2)}) copy-start(f32[64,64]{1,0:T(8,128)} %copy-done.8) | copy-start | bytes 49156
  356.6 42.4 %copy-start.14 = (s32[1024]{0:T(1024)S(1)}, s32[1024]{0:T(1024)}, u32[]{:S(2)}) copy-start(s32[1024]{0:T(1024)} %get-tuple-element.648) | copy-start | bytes 12292
  356.6 42.4 %copy-start.21 = (s32[64]{0:T(128)S(1)}, s32[64]{0:T(128)}, u32[]{:S(2)}) copy-start(s32[64]{0:T(128)} %copy-done.20) | copy-start | bytes 772
  399.7 1.0 copy-start.1
where the time goes:
time: 400 us; the launch traced here: 402 us
  Pallas kernels  331 us (83%)
  local copies, waits for them, and re-layouts  27.9 us (7%)
  other arithmetic  25.3 us (6%)
  matrix products  13.4 us (3%)
    pallas_call x1, Pallas kernels, axis_sum(): pl.pallas_call(kernel, out_shape=same, in_specs=[VMEM] * len(same), out_s...  84.5 us
    pallas_call x1, Pallas kernels, softmax(): pl.pallas_call(kernel, out_shape=[jax.ShapeDtypeStruct((n_cand, width), f...  54.9 us
    pallas_call x1, Pallas kernels, fetch(): pl.pallas_call(kernel, out_shape=[jax.ShapeDtypeStruct((n_row, CAP, width...  48.7 us
    pallas_call x1, Pallas kernels, add_rows(): pl.pallas_call(kernel, out_shape=jax.ShapeDtypeStruct((n_rows, width), jn...  42.4 us
    pallas_call x1, Pallas kernels, core_sum(): pl.pallas_call(kernel, out_shape=[jax.ShapeDtypeStruct(lead + (n, width),...  35.1 us
    pallas_call x1, Pallas kernels, gather_cands(): pl.pallas_call(kernel, out_shape=[jax.ShapeDtypeStruct((n_dp * n_row, chu...  30.6 us
    pallas_call x1, Pallas kernels, core_swap(): pl.pallas_call(kernel, out_shape=[jax.ShapeDtypeStruct((n_dp,) + x.shape,...  25.7 us
    reduce_sum x2, other arithmetic, to_slots(): jnp.sum(jnp.where(hit, v[:, None], jnp.zeros((), v.dtype)), axis=0)  9.7 us

commit v1 on v0

--- a/solution.py
+++ b/solution.py
@@ -9,17 +9,30 @@
 
 ALL_AXES = ("dp", "row")
 MESH = pl.DeviceIdType.MESH
-CAP = 96
-BLK = 512
-TOK = 256
+CAP = 112
+BLK = 2048
+TOK = 512
 LANES = 128
 ANY = pl.BlockSpec(memory_space=pl.ANY)
 VMEM = pl.BlockSpec(memory_space=pltpu.VMEM)
 SMEM = pl.BlockSpec(memory_space=pltpu.SMEM)
 
 
-def params():
-    return pltpu.CompilerParams(has_side_effects=True, vmem_limit_bytes=60 * 1024 * 1024)
+def params(barrier=None):
+    return pltpu.CompilerParams(has_side_effects=True, vmem_limit_bytes=60 * 1024 * 1024, collective_id=barrier)
+
+
+def greet(n_row, n_dp, rows, partner):
+    row, dp = lax.axis_index("row"), lax.axis_index("dp")
+    barrier = pltpu.get_barrier_semaphore()
+    if partner:
+        pl.semaphore_signal(barrier, inc=1, device_id={"row": row, "dp": lax.rem(dp + 1, n_dp)}, device_id_type=MESH)
+    if rows:
+        def one(j, carry):
+            pl.semaphore_signal(barrier, inc=1, device_id={"row": lax.rem(row + j, n_row), "dp": dp}, device_id_type=MESH)
+            return carry
+        lax.fori_loop(1, n_row, one, 0)
+    pl.semaphore_wait(barrier, (n_row - 1 if rows else 0) + (1 if partner else 0))
 
 
 def exchange(n_row, n_dp, both, *xs):
@@ -109,6 +122,7 @@
             return pltpu.make_async_copy(tab_ref.at[sl], tab16.at[p], tab_sem.at[p])
         load(0, 0).start()
         load(1, 1).start()
+        greet(n_row, n_dp, True, False)
         pltpu.make_async_copy(want_ref.at[row], asked.at[row], sems.at[1]).start()
 
         def ask(j, carry):
@@ -146,15 +160,14 @@
                 stage[pl.ds(c, 1), :] = tab32[pl.ds(ask_s[peer, 0, c], 1), :]
             out_buf[peer] = stage[...].astype(jnp.bfloat16)
 
-        gather(1)
-
         def step(j, carry):
             gather(j)
-            send(lax.rem(row + j - 1, n_row))
+
+            @pl.when(j > 1)
+            def _():
+                send(lax.rem(row + j - 1, n_row))
             return carry
-        lax.fori_loop(2, n_row, step, 0)
-        gather(n_row)
-        send(lax.rem(row + n_row - 1, n_row))
+        lax.fori_loop(1, n_row + 1, step, 0)
         pltpu.make_async_copy(out_buf.at[row], rows_ref.at[row], sems.at[3]).start()
         sent = want_ref.at[pl.ds(0, n_row - 1)]
         pltpu.make_async_copy(sent, sent, sems.at[0]).wait()
@@ -180,17 +193,20 @@
             pltpu.SemaphoreType.DMA((4,)),
             pltpu.SemaphoreType.DMA((2,)),
         ],
-        compiler_params=params(),
+        compiler_params=params(2),
     )(want, table)
 
 
-def gather_cands(n_row, n_dp, my_cands, most):
-    chunk, width = my_cands.shape
-
-    def kernel(mine_ref, most_ref, all_ref, top_ref, theirs, sems):
+def gather_cands(n_row, n_dp, got, n_tok, most):
+    chunk, width = got.shape[0] - n_tok, got.shape[1]
+
+    def kernel(got_ref, most_ref, all_ref, top_ref, theirs, sems):
+        mine_ref = got_ref.at[pl.ds(n_tok, chunk)]
         row, dp = lax.axis_index("row"), lax.axis_index("dp")
         other = lax.rem(dp + 1, n_dp)
         me = dp * n_row + row
+
+        greet(n_row, n_dp, True, True)
 
         def one(j, carry):
             peer = lax.rem(row + j, n_row)
@@ -219,14 +235,14 @@
     return pl.pallas_call(
         kernel,
         out_shape=[
-            jax.ShapeDtypeStruct((n_dp * n_row, chunk, width), my_cands.dtype),
+            jax.ShapeDtypeStruct((n_dp * n_row, chunk, width), got.dtype),
             jax.ShapeDtypeStruct(most.shape, most.dtype),
         ],
         in_specs=[VMEM, VMEM],
         out_specs=[VMEM, VMEM],
         scratch_shapes=[pltpu.VMEM(most.shape, most.dtype), pltpu.SemaphoreType.DMA((6,))],
-        compiler_params=params(),
-    )(my_cands, most)
+        compiler_params=params(3),
+    )(got, most)
 
 
 def softmax(n_total, cand_rows, hidden, tgt, y_lanes, cand_ids, log_q):
@@ -361,6 +377,7 @@
                 src_ref=src.at[other], dst_ref=dst, send_sem=sems.at[i, 0], recv_sem=sems.at[i, 1],
                 device_id={"row": row, "dp": other}, device_id_type=MESH)
             for i, (src, dst) in enumerate(((cand_ref, cand_in), (rest_ref, rest_in)))]
+        greet(n_row, n_dp, False, True)
         for c in copies:
             c.start()
         for c in copies:
@@ -388,11 +405,11 @@
             pltpu.VMEM(rest.shape[1:], jnp.float32),
             pltpu.SemaphoreType.DMA((2, 2)),
         ],
-        compiler_params=params(),
+        compiler_params=params(0),
     )(cand, rest)
 
 
-def axis_sum(side, parts, moved):
+def axis_sum(side, n_dp, parts, moved):
     n_row = side ** 3
     n_p, n_m = len(parts), len(moved)
     f32 = jnp.float32
@@ -407,6 +424,7 @@
         row, dp = lax.axis_index("row"), lax.axis_index("dp")
         z, y, x = coords(row, side)
         at = [order(p, z, y, x) for p in range(n_p)]
+        greet(n_row, n_dp, True, False)
 
         def send(p, phase, axis, k, src, dst):
             to = list(at[p])
@@ -493,7 +511,7 @@
         out_specs=[VMEM] * len(same),
         scratch_shapes=[v for group in scratch for v in group] + [
             pltpu.SemaphoreType.DMA((n_p, 6, 2)), pltpu.SemaphoreType.DMA((n_m, 2))],
-        compiler_params=params(),
+        compiler_params=params(4),
     )(*parts, *moved)
 
 
@@ -510,6 +528,7 @@
                 src_ref=ins[i], dst_ref=outs[i].at[dp], send_sem=sems.at[i, 0], recv_sem=sems.at[i, 1],
                 device_id={"row": row, "dp": other}, device_id_type=MESH))
             copies.append(pltpu.make_async_copy(ins[i], outs[i].at[dp], sems.at[i, 2]))
+        greet(1, n_dp, False, True)
         for c in copies:
             c.start()
         for c in copies:
@@ -521,7 +540,7 @@
         in_specs=[VMEM] * n,
         out_specs=[VMEM] * n,
         scratch_shapes=[pltpu.SemaphoreType.DMA((n, 3))],
-        compiler_params=params(),
+        compiler_params=params(1),
     )(*xs)
 
 
@@ -530,9 +549,9 @@
     n_full = n_rows + 8
     chunk = min(128, n_rows)
     flat, specs = [], []
-    for row_ids, counts, vals, val_ids in groups:
-        flat += [row_ids, counts, vals] + ([] if val_ids is None else [val_ids])
-        specs += [SMEM, SMEM, VMEM] + ([] if val_ids is None else [SMEM])
+    for row_ids, counts, vals, extra in groups:
+        flat += [row_ids, counts, vals, extra]
+        specs += [SMEM, SMEM, VMEM, SMEM]
     if grad is not None:
         flat.append(grad)
         specs.append(ANY)
@@ -540,12 +559,19 @@
     def kernel(*refs):
         refs = list(refs)
         work = []
-        for _, _, vals, val_ids in groups:
-            idx, cnt, ref = refs.pop(0), refs.pop(0), refs.pop(0)
-            work.append((idx, cnt, ref, None if val_ids is None else refs.pop(0)))
+        for _ in groups:
+            work.append([refs.pop(0) for _ in range(4)])
         grad_ref = refs.pop(0) if grad is not None else None
-        out_ref, sem = refs[0], refs[-1]
-        accs = refs[1:-1]
+        out_ref, wide, sem = refs[0], refs[-2], refs[-1]
+        accs = refs[1:-2]
+        hid_ref = work[0][2]
+        part = hid_ref.shape[0] // (groups[0][0].shape[0] // 2)
+
+        def widen(k, carry):
+            sl = pl.ds(pl.multiple_of(k * part, part), part)
+            wide[sl, :] = hid_ref[sl, :].astype(jnp.float32)
+            return carry
+        lax.fori_loop(0, hid_ref.shape[0] // part, widen, 0)
         if grad_ref is not None:
             cp_in = pltpu.make_async_copy(grad_ref, accs[0].at[pl.ds(0, n_rows)], sem)
             cp_in.start()
@@ -562,17 +588,19 @@
         if grad_ref is not None:
             cp_in.wait()
 
-        for idx, cnt, vals_ref, vid in work:
+        for which, (idx, cnt, vals_ref, extra) in enumerate(work):
             per_list = vals_ref.shape[0] // idx.shape[0]
 
-            def one_list(i, carry, idx=idx, cnt=cnt, vals_ref=vals_ref, vid=vid, per_list=per_list):
+            def one_list(i, carry, which=which, idx=idx, cnt=cnt, vals_ref=vals_ref, extra=extra, per_list=per_list):
                 def group(q, c2):
                     for u in range(8):
                         c = q * 8 + u
                         acc = accs[u % n_acc]
                         r = idx[i, c]
-                        v = i * per_list + c if vid is None else vid[i, c]
-                        acc[pl.ds(r, 1), :] += vals_ref[pl.ds(v, 1), :]
+                        if which == 0:
+                            acc[pl.ds(r, 1), :] += extra[i, c] * wide[pl.ds(i * per_list + c, 1), :]
+                        else:
+                            acc[pl.ds(r, 1), :] += vals_ref[pl.ds(extra[i, c], 1), :]
                     return c2
                 return lax.fori_loop(0, (cnt[i] + 7) // 8, group, carry)
             lax.fori_loop(0, idx.shape[0], one_list, 0)
@@ -595,7 +623,8 @@
         out_shape=jax.ShapeDtypeStruct((n_rows, width), jnp.float32),
         in_specs=specs,
         out_specs=ANY,
-        scratch_shapes=[pltpu.VMEM((n_full, width), jnp.float32)] * n_acc + [pltpu.SemaphoreType.DMA],
+        scratch_shapes=[pltpu.VMEM((n_full, width), jnp.float32)] * n_acc + [
+            pltpu.VMEM(groups[0][2].shape, jnp.float32), pltpu.SemaphoreType.DMA],
         compiler_params=pltpu.CompilerParams(vmem_limit_bytes=60 * 1024 * 1024),
     )(*flat)
 
@@ -666,24 +695,24 @@
                 lane = jnp.arange(LANES)[None, None, :]
                 rows_in, most_all = fetch(n_row, n_dp, jnp.where(lane == LANES - 1, most, want), tab_loc)
                 got = jnp.take(rows_in.reshape(n_row * CAP, width), at, axis=0, mode="clip")
-                return hit, got, hid_out, most_all
-
-            _, got, hid_out, most_dp = fetch_round(0)
-            cand_rows, most_all = gather_cands(n_row, n_dp, got[n_tok:], most_dp)
+                return hit, got, hid_out, want, most_all
+
+            _, got, hid_out, want, most_dp = fetch_round(0)
+            cand_rows, most_all = gather_cands(n_row, n_dp, got, n_tok, most_dp)
             most_all = most_all[0, LANES - 1]
 
             def fetch_more(carry):
                 k, got, _ = carry
-                hit, new, _, most = fetch_round(k)
+                hit, new, _, _, most = fetch_round(k)
                 got = jnp.where(hit[:, None], new, got)
-                return k + 1, got, gather_cands(n_row, n_dp, got[n_tok:], most)[0]
+                return k + 1, got, gather_cands(n_row, n_dp, got, n_tok, most)[0]
 
             _, got, cand_rows = lax.while_loop(
                 lambda c: c[0] * CAP < most_all, fetch_more, (jnp.int32(1), got, cand_rows))
-            tgt_rows, cand_rows = got[:n_tok], cand_rows.reshape(n_cand, width)
+            cand_rows = cand_rows.reshape(n_cand, width)
 
             cand_grad, grad_hid, dz_lanes, loss_part = softmax(
-                n_total, cand_rows, hidden, tgt_rows,
+                n_total, cand_rows, hidden, got,
                 jnp.broadcast_to(y_loc[:, None], (n_tok, LANES)), cand_ids[None, :], log_q[None, :])
             dz_tgt, loss_sum = dz_lanes[:, 0], loss_part[0, 0]
 
@@ -692,7 +721,7 @@
             grad_pre = gelu_vjp(grad_act)[0].astype(bf16)
             grad_up = jnp.einsum("ti,tf->if", x_loc, grad_pre, preferred_element_type=f32)
 
-            t_rank, t_owner, t_local = rank[:n_tok], owner[:n_tok], local[:n_tok]
+            t_rank, t_owner = rank[:n_tok], owner[:n_tok]
             t_count = jnp.sum((t_owner[:, None] == jnp.arange(n_row)[None, :]).astype(jnp.int32), axis=0)
             c_rank, _ = ranks(owner[n_tok:], n_row)
             c_slot = owner[n_tok:] * chunk + c_rank
@@ -707,10 +736,11 @@
                 first.append((((part * n_dp + dp) * n_row + (a * side + b) * side + c) * half).astype(f32))
             c_pos = jnp.where(c_pos < half, first[0] + c_pos, first[1] + c_pos - half)
 
-            def give(k):
+            def give(k, want):
                 rel = t_rank - k * CAP
                 slot = jnp.where((rel >= 0) & (rel < CAP), t_owner * CAP + rel, -1)
-                t_row, t_dz = to_slots(slot, [t_local.astype(f32), dz_tgt], n_row * CAP)
+                (t_dz,) = to_slots(slot, [dz_tgt], n_row * CAP)
+                t_row = want[:, 0, :CAP].astype(f32)
                 now = jnp.clip(t_count - k * CAP, 0, CAP).astype(f32)
                 counts = jnp.stack([now, c_count.astype(f32), jnp.full((n_row,), loss_sum)], axis=1)
                 return tile_rows([t_row.reshape(n_row, CAP), t_dz.reshape(n_row, CAP), c_row, c_pos, counts], n_row)
@@ -718,8 +748,7 @@
             to_int = lambda v: v.astype(jnp.int32)
 
             def token_group(hid_in, meta_in):
-                vals = meta_in[:, 1, :CAP, None] * hid_in.astype(f32)
-                return to_int(meta_in[:, 0, :CAP]), to_int(meta_in[:, 4, 0]), vals.reshape(n_dev * CAP, width), None
+                return to_int(meta_in[:, 0, :CAP]), to_int(meta_in[:, 4, 0]), hid_in.reshape(n_dev * CAP, width), meta_in[:, 1, :CAP]
 
             blocks = w_up.shape[1] // LANES
             up_shape = (n_dev // blocks, w_up.shape[0] * blocks // n_dev, blocks, LANES)
@@ -727,7 +756,7 @@
                 grad_up.reshape(up_shape).transpose(0, 2, 1, 3).reshape(n_dp, n_row, up_shape[1], width),
                 grad_down.reshape(n_dp, n_row, -1, width)], axis=2)
             parts = core_sum(side, cand_grad.reshape(n_dp, n_row, 2, half, width), rest)
-            g0, g1, g2, hid_in, meta_in = axis_sum(side, parts, [hid_out, give(0)])
+            g0, g1, g2, hid_in, meta_in = axis_sum(side, n_dp, parts, [hid_out, give(0, want)])
             g0, g1, g2, hid_in, meta_in = core_swap(n_dp, g0, g1, g2, hid_in, meta_in)
             hid_in, meta_in = hid_in.reshape(n_dev, CAP, width), meta_in.reshape(n_dev, 8, LANES)
             cand_sums = jnp.concatenate([g0.reshape(-1, width), g1.reshape(-1, width)], axis=0)
@@ -741,7 +770,8 @@
 
             def give_more(carry):
                 k, grad = carry
-                return k + 1, add_rows(rows_local, [token_group(*exchange(n_row, n_dp, True, pack_round(k)[2], give(k)))], grad, 1)
+                _, _, hid_more, want_more = pack_round(k)
+                return k + 1, add_rows(rows_local, [token_group(*exchange(n_row, n_dp, True, hid_more, give(k, want_more)))], grad, 1)
 
             _, grad = lax.while_loop(lambda c: c[0] * CAP < most_all, give_more, (jnp.int32(1), grad))
             return jnp.sum(meta_in[:, 4, 2]) / n_total, grad, grad_up, grad_down

time: 400 us -> 352 us (0.88)
  the two profiles are of different devices: /device:TPU:1 before, /device:TPU:15 now
where the time goes in v1:
time: 352 us; the launch traced here: 347 us
  Pallas kernels  277 us (79%)
  other arithmetic  26 us (7%)
  local copies, waits for them, and re-layouts  24.7 us (7%)
  matrix products  14.4 us (4%)
    pallas_call x1, Pallas kernels, axis_sum(): pl.pallas_call(kernel, out_shape=same, in_specs=[VMEM] * len(same), out_s...  84.8 us
    pallas_call x1, Pallas kernels, add_rows(): pl.pallas_call(kernel, out_shape=jax.ShapeDtypeStruct((n_rows, width), jn...  46.5 us
    pallas_call x1, Pallas kernels, fetch(): pl.pallas_call(kernel, out_shape=[jax.ShapeDtypeStruct((n_row, CAP, width...  46.1 us
    pallas_call x1, Pallas kernels, softmax(): pl.pallas_call(kernel, out_shape=[jax.ShapeDtypeStruct((n_cand, width), f...  36.7 us
    pallas_call x1, Pallas kernels, gather_cands(): pl.pallas_call(kernel, out_shape=[jax.ShapeDtypeStruct((n_dp * n_row, chu...  26.4 us
    pallas_call x1, Pallas kernels, core_swap(): pl.pallas_call(kernel, out_shape=[jax.ShapeDtypeStruct((n_dp,) + x.shape,...  16.5 us
    reduce_sum x2, other arithmetic, to_slots(): jnp.sum(jnp.where(hit, v[:, None], jnp.zeros((), v.dtype)), axis=0)  13.3 us
    pallas_call x1, Pallas kernels, core_sum(): pl.pallas_call(kernel, out_shape=[jax.ShapeDtypeStruct(lead + (n, width),...  10.8 us

profile of v1, /device:TPU:15, one launch (start us, length us, event | category | flops | bytes accessed | tf_op | source)
XLA Modules:
  0.0 346.5 jit_solution(14915937583609566077)
XLA Ops:
  0.7 0.8 dynamic_slice.3
  1.5 0.8 dynamic-slice_bitcast_fusion
  6.1 1.2 convert_bitcast_fusion.2
  10.1 1.7 broadcast_in_dim.162.y_ref
  11.8 4.5 %multiply_convert_fusion = (bf16[1024,1024]{1,0:T(8,128)(2,1)S(1)}, f32[1024,1024]{1,0:T(8,128)}) fusion(bf16[1024,256]{1,0:T(8,128)(2,1)S(1)} %copy-done, bf16[256,1024]{1,0:T(8,128)(2,1)} %param.12), kind=kOutput, calls=%fused_computation.35 | convolution fusion | flops 546308096 | bytes 7340032 | tf_op jit(solution)/shard_map/dot_general | solution.py:678
  17.7 8.8 %shard_map.102 = (bf16[64,112,128]{2,1,0:T(8,128)(2,1)S(1)}, s32[64,1,128]{2,1,0:T(1,128)S(1)}) custom-call(s32[1,1152]{1,0:T(1,128)S(1)} %broadcast_in_dim.161.slot_ref, bf16[1152,256]{1,0:T(8,128)(2,1)S(1)} %fusion.17.vals_ref), custom_call_target="tpu_custom_call" | custom-call | tf_op jit(solution)/shard_map/pallas_call | solution.py:96
  26.5 1.3 copy-done.3
  27.8 1.3 broadcast_select_fusion.2.want_ref
  29.7 46.1 %shard_map.103 = (bf16[64,112,128]{2,1,0:T(8,128)(2,1)}, s32[8,128]{1,0:T(8,128)}) custom-call(s32[64,1,128]{2,1,0:T(1,128)} %broadcast_select_fusion.2.want_ref, bf16[16384,128]{1,0:T(8,128)(2,1)} %tab_ref.1), custom_call_target="tpu_custom_call" | custom-call | tf_op jit(solution)/shard_map/pallas_call | solution.py:178
  75.8 4.2 %gather_fusion.1 = bf16[1088,128]{1,0:T(8,128)(2,1)S(1)} fusion(bf16[7168,128]{1,0:T(8,128)(2,1)} %bitcast.131, s32[2048]{0:T(1024)S(1)} %pad_clamp_fusion.1), kind=kCustom, calls=%fused_computation.1 | custom fusion | bytes 561408 | tf_op jit(solution)/shard_map/jit(_take)/gather | solution.py:697
  80.0 26.4 %shard_map.104 = (bf16[128,64,128]{2,1,0:T(8,128)(2,1)}, s32[8,128]{1,0:T(8,128)}) custom-call(bf16[1088,128]{1,0:T(8,128)(2,1)S(1)} %gather_fusion.1, s32[8,128]{1,0:T(8,128)} %get-tuple-element.260.most_ref), custom_call_target="tpu_custom_call" | custom-call | tf_op jit(solution)/shard_map/pallas_call | solution.py:235
  106.4 1.3 slice.76
  107.8 0.9 while.24
  108.7 36.7 %shard_map.105 = (f32[8192,128]{1,0:T(8,128)}, bf16[1024,128]{1,0:T(8,128)(2,1)}, f32[1024,128]{1,0:T(8,128)}, f32[8,128]{1,0:T(8,128)}) custom-call(bf16[8192,128]{1,0:T(8,128)(2,1)} %bitcast.132, bf16[1024,128]{1,0:T(8,128)(2,1)} %copy-done.6, bf16[1088,128]{1,0:T(8,128)(2,1)S(1)} %get-tuple-element.264.t_ref, s32[1024,128]{1,0:T(8,128)} %broadcast_in_dim.162.y_ref, ...), custom_call_target="tpu_custom_call" | custom-call | tf_op jit(solution)/shard_map/pallas_call | solution.py:333
  145.4 6.7 %fusion.12 = f32[256,1024]{0,1:T(8,128)} fusion(bf16[1024,256]{1,0:T(8,128)(2,1)S(1)} %copy-done, f32[1024,1024]{1,0:T(8,128)} %get-tuple-element.413, bf16[1024,128]{1,0:T(8,128)(2,1)} %get-tuple-element.266, bf16[1024,128]{1,0:T(8,128)(2,1)S(1)} %copy-done.10), kind=kOutput, calls=%fused_computation.39 | convolution fusion | flops 826277888 | bytes 6291456 | tf_op jit(solution)/shard_map/ti,tf->if/dot_general | solution.py:722
  152.1 1.7 fusion.43
  153.8 1.6 copy.63
  155.9 1.2 pad_maximum_fusion.1.rest_ref
  157.1 1.2 slice.83
  158.4 10.8 %shard_map.106 = (f32[4,4,4,32,128]{4,3,2,1,0:T(8,128)}, f32[4,4,4,32,128]{4,3,2,1,0:T(8,128)}, f32[4,4,4,24,128]{4,3,2,1,0:T(8,128)}) custom-call(f32[2,64,2,32,128]{4,3,2,1,0:T(8,128)} %bitcast.119, f32[2,64,24,128]{3,2,1,0:T(8,128)} %pad_maximum_fusion.1.rest_ref), custom_call_target="tpu_custom_call" | custom-call | tf_op jit(solution)/shard_map/pallas_call | solution.py:398
  170.5 13.0 %select_reduce_fusion.1 = f32[7168]{0:T(1024)S(1)} fusion(f32[1024]{0:T(1024)S(1)} %get-tuple-element.399, s32[1024]{0:T(1024)S(1)} %copy-done.18), kind=kLoop, calls=%fused_computation.21 | loop fusion | flops 22012928 | bytes 36864 | tf_op jit(solution)/shard_map/reduce_sum | solution.py:644
  183.7 1.0 stack.77.refs_4_
  184.7 84.8 %shard_map.107 = (f32[4,4,4,32,128]{4,3,2,1,0:T(8,128)}, f32[4,4,4,32,128]{4,3,2,1,0:T(8,128)}, f32[4,4,4,24,128]{4,3,2,1,0:T(8,128)}, bf16[64,112,128]{2,1,0:T(8,128)(2,1)}, f32[64,8,128]{2,1,0:T(8,128)}) custom-call(f32[4,4,4,32,128]{4,3,2,1,0:T(8,128)} %get-tuple-element.267.refs_0_, f32[4,4,4,32,128]{4,3,2,1,0:T(8,128)} %get-tuple-element.268.refs_1_, ...), custom_call_target="tpu_custom_call" | custom-call | tf_op jit(solution)/shard_map/pallas_call | solution.py:507
  269.5 16.5 %shard_map.108 = (f32[2,4,4,4,32,128]{5,4,3,2,1,0:T(8,128)}, f32[2,4,4,4,32,128]{5,4,3,2,1,0:T(8,128)}, f32[2,4,4,4,24,128]{5,4,3,2,1,0:T(8,128)}, bf16[2,64,112,128]{3,2,1,0:T(8,128)(2,1)}, f32[2,64,8,128]{3,2,1,0:T(8,128)}) custom-call(f32[4,4,4,32,128]{4,3,2,1,0:T(8,128)} %get-tuple-element.273.refs_0_, f32[4,4,4,32,128]{4,3,2,1,0:T(8,128)} %get-tuple-element.274.refs_1_, ...), custom_call_target="tpu_custom_call" | custom-call | tf_op jit(solution)/shard_map/pallas_call | solution.py:537
  286.0 1.1 copy.67
  288.5 0.8 fusion.21
  290.6 1.6 copy.69
  292.2 0.8 slice_bitcast_fusion.1
  293.5 1.2 copy.75
  294.7 2.2 pad_maximum_fusion.refs_6_
  296.9 46.5 %shard_map.109 = f32[16384,128]{1,0:T(8,128)} custom-call(s32[128,112]{1,0:T(8,128)} %get-tuple-element.403.refs_0_, s32[128]{0:T(128)} %get-tuple-element.341.refs_1_, bf16[14336,128]{1,0:T(8,128)(2,1)} %bitcast.125, f32[128,112]{1,0:T(8,128)} %get-tuple-element.402.refs_3_, s32[128,64]{1,0:T(8,128)} %get-tuple-element.401.refs_4_, ...), custom_call_target="tpu_custom_call" | custom-call | tf_op jit(solution)/shard_map/pallas_call | solution.py:621
  344.2 1.0 copy-done.1
  (90 shorter events, 13.6 us)
Async XLA Ops:
  0.6 11.1 %copy-start = (bf16[1024,256]{1,0:T(8,128)(2,1)S(1)}, bf16[1024,256]{1,0:T(8,128)(2,1)}, u32[]{:S(2)}) copy-start(bf16[1024,256]{1,0:T(8,128)(2,1)} %param.11) | copy-start | bytes 1572868
  6.0 2.5 copy-start.11
  6.1 1.2 copy-start.19
  11.8 4.5 %copy-start.10 = (bf16[1024,128]{1,0:T(8,128)(2,1)S(1)}, bf16[1024,128]{1,0:T(8,128)(2,1)}, u32[]{:S(2)}) copy-start(bf16[1024,128]{1,0:T(8,128)(2,1)} %param.13) | copy-start | bytes 786436
  16.3 1.3 copy-start.4
  17.6 62.4 %copy-start.6 = (bf16[1024,128]{1,0:T(8,128)(2,1)}, bf16[1024,128]{1,0:T(8,128)(2,1)S(1)}, u32[]{:S(2)}) copy-start(bf16[1024,128]{1,0:T(8,128)(2,1)S(1)} %convolution_convert_fusion.h_ref) | copy-start | bytes 786436
  26.5 1.3 copy-start.3
  145.4 6.7 %copy-start.5 = (bf16[1024,1024]{1,0:T(8,128)(2,1)S(1)}, bf16[1024,1024]{1,0:T(8,128)(2,1)}, u32[]{:S(2)}) copy-start(bf16[1024,1024]{1,0:T(8,128)(2,1)} %copy-done.4) | copy-start | bytes 6291460
  155.8 14.1 %copy-start.17 = (f32[64,1]{0,1:T(1,128)S(1)}, f32[64,1]{0,1:T(1,128)}, u32[]{:S(2)}) copy-start(f32[64,1]{0,1:T(1,128)} %get-tuple-element.629) | copy-start | bytes 772
  155.9 14.1 %copy-start.21 = (f32[64,1]{0,1:T(1,128)S(1)}, f32[64,1]{0,1:T(1,128)}, u32[]{:S(2)}) copy-start(f32[64,1]{0,1:T(1,128)} %get-tuple-element.409) | copy-start | bytes 772
  155.9 14.2 %copy-start.9 = (f32[1024,128]{1,0:T(8,128)S(1)}, f32[1024,128]{1,0:T(8,128)}, u32[]{:S(2)}) copy-start(f32[1024,128]{1,0:T(8,128)} %get-tuple-element.271) | copy-start | bytes 1572868
  157.1 13.4 %copy-start.18 = (s32[1024]{0:T(1024)S(1)}, s32[1024]{0:T(1024)}, u32[]{:S(2)}) copy-start(s32[1024]{0:T(1024)} %get-tuple-element.405) | copy-start | bytes 12292
  157.1 26.6 %copy-start.14 = (f32[64,128]{1,0:T(8,128)S(1)}, f32[64,128]{1,0:T(8,128)}, u32[]{:S(2)}) copy-start(f32[64,128]{1,0:T(8,128)} %pad.78) | copy-start | bytes 98308
  157.1 26.6 %copy-start.15 = (f32[64,128]{1,0:T(8,128)S(1)}, f32[64,128]{1,0:T(8,128)}, u32[]{:S(2)}) copy-start(f32[64,128]{1,0:T(8,128)} %pad.79) | copy-start | bytes 98308
  157.1 26.6 %copy-start.16 = (f32[64,128]{1,0:T(8,128)S(1)}, f32[64,128]{1,0:T(8,128)}, u32[]{:S(2)}) copy-start(f32[64,128]{1,0:T(8,128)} %pad.76) | copy-start | bytes 98308
  292.2 2.4 copy-start.7
  292.2 2.4 copy-start.8
  296.9 46.6 %copy-start.12 = (s32[1024]{0:T(1024)S(1)}, s32[1024]{0:T(1024)}, u32[]{:S(2)}) copy-start(s32[1024]{0:T(1024)} %copy-done.11) | copy-start | bytes 12292
  296.9 46.6 %copy-start.13 = (s32[1024]{0:T(1024)S(1)}, s32[1024]{0:T(1024)}, u32[]{:S(2)}) copy-start(s32[1024]{0:T(1024)} %get-tuple-element.622) | copy-start | bytes 12292
  296.9 46.6 %copy-start.20 = (s32[64]{0:T(128)S(1)}, s32[64]{0:T(128)}, u32[]{:S(2)}) copy-start(s32[64]{0:T(128)} %copy-done.19) | copy-start | bytes 772
  344.2 1.0 copy-start.1

commit v2 on v1

--- a/solution.py
+++ b/solution.py
@@ -11,7 +11,7 @@
 MESH = pl.DeviceIdType.MESH
 CAP = 112
 BLK = 2048
-TOK = 512
+TOK = 256
 LANES = 128
 ANY = pl.BlockSpec(memory_space=pl.ANY)
 VMEM = pl.BlockSpec(memory_space=pltpu.VMEM)
@@ -107,6 +107,36 @@
         ],
         compiler_params=pltpu.CompilerParams(vmem_limit_bytes=40 * 1024 * 1024),
     )(slot_row, vals)
+
+
+def place(base, slot_lanes, dz_lanes):
+    n_row, n_tok = base.shape[0], dz_lanes.shape[0]
+    per, step = 4, 64
+
+    def kernel(base_ref, slot_ref, dz_ref, out_ref):
+        first = pl.program_id(0) * per
+        lane = lax.broadcasted_iota(jnp.int32, (step, LANES), 1)
+
+        def some(k, sums):
+            sl = pl.ds(pl.multiple_of(k * step, step), step)
+            slot, dz = slot_ref[sl, :] - first * LANES - lane, dz_ref[sl, :]
+            picked = [jnp.where(slot == o * LANES, dz, 0.0).reshape(step // 8, 8, LANES) for o in range(per)]
+            return tuple(s + jnp.sum(v, axis=0) for s, v in zip(sums, picked))
+        sums = lax.fori_loop(0, n_tok // step, some, (jnp.zeros((8, LANES), jnp.float32),) * per)
+        which = lax.broadcasted_iota(jnp.int32, (8, LANES), 0)
+        for o in range(per):
+            out_ref[o] = base_ref[o] + jnp.where(which == 1, jnp.sum(sums[o], axis=0, keepdims=True), 0.0)
+
+    tile = pl.BlockSpec((per, 8, LANES), lambda i: (i, 0, 0))
+    whole = pl.BlockSpec((n_tok, LANES), lambda i: (0, 0))
+    return pl.pallas_call(
+        kernel,
+        grid=(n_row // per,),
+        out_shape=jax.ShapeDtypeStruct(base.shape, base.dtype),
+        in_specs=[tile, whole, whole],
+        out_specs=tile,
+        compiler_params=pltpu.CompilerParams(vmem_limit_bytes=40 * 1024 * 1024),
+    )(base, slot_lanes, dz_lanes)
 
 
 def fetch(n_row, n_dp, want, table):
@@ -515,19 +545,21 @@
     )(*parts, *moved)
 
 
-def core_swap(n_dp, *xs):
-    n = len(xs)
+def core_swap(n_dp, *groups):
+    flat = [x for group in groups for x in group]
+    n, n_out = len(flat), len(groups)
+    where = [(o, p) for o, group in enumerate(groups) for p in range(len(group))]
 
     def kernel(*refs):
-        ins, outs, sems = refs[:n], refs[n:2 * n], refs[2 * n]
+        ins, outs, sems = refs[:n], refs[n:n + n_out], refs[n + n_out]
         row, dp = lax.axis_index("row"), lax.axis_index("dp")
         other = lax.rem(dp + 1, n_dp)
         copies = []
-        for i in range(n):
+        for i, (o, p) in enumerate(where):
             copies.append(pltpu.make_async_remote_copy(
-                src_ref=ins[i], dst_ref=outs[i].at[dp], send_sem=sems.at[i, 0], recv_sem=sems.at[i, 1],
+                src_ref=ins[i], dst_ref=outs[o].at[p, dp], send_sem=sems.at[i, 0], recv_sem=sems.at[i, 1],
                 device_id={"row": row, "dp": other}, device_id_type=MESH))
-            copies.append(pltpu.make_async_copy(ins[i], outs[i].at[dp], sems.at[i, 2]))
+            copies.append(pltpu.make_async_copy(ins[i], outs[o].at[p, dp], sems.at[i, 2]))
         greet(1, n_dp, False, True)
         for c in copies:
             c.start()
@@ -536,18 +568,19 @@
 
     return pl.pallas_call(
         kernel,
-        out_shape=[jax.ShapeDtypeStruct((n_dp,) + x.shape, x.dtype) for x in xs],
+        out_shape=[jax.ShapeDtypeStruct((len(g), n_dp) + g[0].shape, g[0].dtype) for g in groups],
         in_specs=[VMEM] * n,
-        out_specs=[VMEM] * n,
+        out_specs=[VMEM] * n_out,
         scratch_shapes=[pltpu.SemaphoreType.DMA((n, 3))],
         compiler_params=params(1),
-    )(*xs)
+    )(*flat)
 
 
 def add_rows(n_rows, groups, grad=None, n_acc=4):
     width = groups[0][2].shape[1]
     n_full = n_rows + 8
     chunk = min(128, n_rows)
+    cut = min(128, n_rows // 8)
     flat, specs = [], []
     for row_ids, counts, vals, extra in groups:
         flat += [row_ids, counts, vals, extra]
@@ -562,8 +595,8 @@
         for _ in groups:
             work.append([refs.pop(0) for _ in range(4)])
         grad_ref = refs.pop(0) if grad is not None else None
-        out_ref, wide, sem = refs[0], refs[-2], refs[-1]
-        accs = refs[1:-2]
+        out_ref, wide, sem, out_sem = refs[0], refs[-3], refs[-2], refs[-1]
+        accs = refs[1:-3]
         hid_ref = work[0][2]
         part = hid_ref.shape[0] // (groups[0][0].shape[0] // 2)
 
@@ -605,18 +638,30 @@
                 return lax.fori_loop(0, (cnt[i] + 7) // 8, group, carry)
             lax.fori_loop(0, idx.shape[0], one_list, 0)
 
-        if n_acc > 1:
-            def merge(k, carry):
-                sl = pl.ds(pl.multiple_of(k * chunk, chunk), chunk)
-                tot = accs[0][sl, :]
-                for a in accs[1:]:
-                    tot = tot + a[sl, :]
-                accs[0][sl, :] = tot
-                return carry
-            lax.fori_loop(0, n_rows // chunk, merge, 0)
-        cp_out = pltpu.make_async_copy(accs[0].at[pl.ds(0, n_rows)], out_ref, sem)
-        cp_out.start()
-        cp_out.wait()
+        piece = n_rows // 8
+
+        def leave(k):
+            sl = pl.ds(pl.multiple_of(k * piece, piece), piece)
+            return pltpu.make_async_copy(accs[0].at[sl], out_ref.at[sl], out_sem.at[k])
+
+        def finish(k, carry):
+            if n_acc > 1:
+                def merge(q, c2):
+                    sl = pl.ds(pl.multiple_of(k * piece + q * cut, cut), cut)
+                    tot = accs[0][sl, :]
+                    for a in accs[1:]:
+                        tot = tot + a[sl, :]
+                    accs[0][sl, :] = tot
+                    return c2
+                lax.fori_loop(0, piece // cut, merge, 0)
+
+            @pl.when(k > 0)
+            def _():
+                leave(k - 1).start()
+            return carry
+        lax.fori_loop(0, 8, finish, 0)
+        leave(7).start()
+        lax.fori_loop(0, 8, lambda k, c: (leave(k).wait(), c)[1], 0)
 
     return pl.pallas_call(
         kernel,
@@ -624,7 +669,7 @@
         in_specs=specs,
         out_specs=ANY,
         scratch_shapes=[pltpu.VMEM((n_full, width), jnp.float32)] * n_acc + [
-            pltpu.VMEM(groups[0][2].shape, jnp.float32), pltpu.SemaphoreType.DMA],
+            pltpu.VMEM(groups[0][2].shape, jnp.float32), pltpu.SemaphoreType.DMA, pltpu.SemaphoreType.DMA((8,))],
         compiler_params=pltpu.CompilerParams(vmem_limit_bytes=60 * 1024 * 1024),
     )(*flat)
 
@@ -714,7 +759,7 @@
             cand_grad, grad_hid, dz_lanes, loss_part = softmax(
                 n_total, cand_rows, hidden, got,
                 jnp.broadcast_to(y_loc[:, None], (n_tok, LANES)), cand_ids[None, :], log_q[None, :])
-            dz_tgt, loss_sum = dz_lanes[:, 0], loss_part[0, 0]
+            loss_sum = loss_part[0, 0]
 
             grad_down = jnp.einsum("tf,td->fd", act_b, grad_hid, preferred_element_type=f32)
             grad_act = jnp.einsum("td,fd->tf", grad_hid, w_down, preferred_element_type=f32)
@@ -738,12 +783,11 @@
 
             def give(k, want):
                 rel = t_rank - k * CAP
-                slot = jnp.where((rel >= 0) & (rel < CAP), t_owner * CAP + rel, -1)
-                (t_dz,) = to_slots(slot, [dz_tgt], n_row * CAP)
-                t_row = want[:, 0, :CAP].astype(f32)
+                slot = jnp.where((rel >= 0) & (rel < CAP), t_owner * LANES + rel, -1)
                 now = jnp.clip(t_count - k * CAP, 0, CAP).astype(f32)
                 counts = jnp.stack([now, c_count.astype(f32), jnp.full((n_row,), loss_sum)], axis=1)
-                return tile_rows([t_row.reshape(n_row, CAP), t_dz.reshape(n_row, CAP), c_row, c_pos, counts], n_row)
+                base = tile_rows([want[:, 0, :CAP].astype(f32), jnp.zeros((n_row, LANES), f32), c_row, c_pos, counts], n_row)
+                return place(base, jnp.broadcast_to(slot[:, None], (n_tok, LANES)), dz_lanes)
 
             to_int = lambda v: v.astype(jnp.int32)
 
@@ -757,10 +801,10 @@
                 grad_down.reshape(n_dp, n_row, -1, width)], axis=2)
             parts = core_sum(side, cand_grad.reshape(n_dp, n_row, 2, half, width), rest)
             g0, g1, g2, hid_in, meta_in = axis_sum(side, n_dp, parts, [hid_out, give(0, want)])
-            g0, g1, g2, hid_in, meta_in = core_swap(n_dp, g0, g1, g2, hid_in, meta_in)
+            cand_sums, g2, hid_in, meta_in = core_swap(n_dp, (g0, g1), (g2,), (hid_in,), (meta_in,))
             hid_in, meta_in = hid_in.reshape(n_dev, CAP, width), meta_in.reshape(n_dev, 8, LANES)
-            cand_sums = jnp.concatenate([g0.reshape(-1, width), g1.reshape(-1, width)], axis=0)
-            rest = jnp.transpose(g2, (0, 1, 3, 2, 4, 5)).reshape(n_dev, -1, width)
+            cand_sums = cand_sums.reshape(n_cand, width)
+            rest = jnp.transpose(g2[0], (0, 1, 3, 2, 4, 5)).reshape(n_dev, -1, width)
             grad_up = rest[:, :up_shape[1]].reshape(up_shape[0], blocks, up_shape[1], LANES).transpose(0, 2, 1, 3).reshape(w_up.shape)
             grad_down = rest[:, up_shape[1]:].reshape(w_down.shape)
 

time: 352 us -> 330 us (0.938)
  the two profiles are of different devices: /device:TPU:15 before, /device:TPU:1 now
where the time goes in v2:
time: 330 us; the launch traced here: 329 us
  Pallas kernels  279 us (85%)
  local copies, waits for them, and re-layouts  21.5 us (7%)
  matrix products  14.9 us (5%)
  other arithmetic  9.63 us (3%)
    pallas_call x1, Pallas kernels, axis_sum(): pl.pallas_call(kernel, out_shape=same, in_specs=[VMEM] * len(same), out_s...  82.2 us
    pallas_call x1, Pallas kernels, fetch(): pl.pallas_call(kernel, out_shape=[jax.ShapeDtypeStruct((n_row, CAP, width...  47.2 us
    pallas_call x1, Pallas kernels, add_rows(): pl.pallas_call(kernel, out_shape=jax.ShapeDtypeStruct((n_rows, width), jn...  44.2 us
    pallas_call x1, Pallas kernels, softmax(): pl.pallas_call(kernel, out_shape=[jax.ShapeDtypeStruct((n_cand, width), f...  38 us
    pallas_call x1, Pallas kernels, gather_cands(): pl.pallas_call(kernel, out_shape=[jax.ShapeDtypeStruct((n_dp * n_row, chu...  27.2 us
    pallas_call x1, Pallas kernels, core_swap(): pl.pallas_call(kernel, out_shape=[jax.ShapeDtypeStruct((len(g), n_dp) + g...  15.4 us
    pallas_call x1, Pallas kernels, core_sum(): pl.pallas_call(kernel, out_shape=[jax.ShapeDtypeStruct(lead + (n, width),...  10.8 us
    pallas_call x1, Pallas kernels, pack(): pl.pallas_call(kernel, grid=(n_row // per,), out_shape=[jax.ShapeDtypeStr...  8.82 us

profile of v2, /device:TPU:1, one launch (start us, length us, event | category | flops | bytes accessed | tf_op | source)
XLA Modules:
  0.0 329.4 jit_solution(5337405139988445731)
XLA Ops:
  0.7 0.8 dynamic_slice.3
  1.5 0.8 dynamic-slice_bitcast_fusion
  4.6 0.7 negate_select_fusion.1
  6.2 0.7 add_reduce_fusion
  7.9 1.7 broadcast_in_dim.134.y_ref
  9.6 4.5 %multiply_convert_fusion = (bf16[1024,1024]{1,0:T(8,128)(2,1)S(1)}, f32[1024,1024]{1,0:T(8,128)}) fusion(bf16[1024,256]{1,0:T(8,128)(2,1)S(1)} %copy-done, bf16[256,1024]{1,0:T(8,128)(2,1)} %param.12), kind=kOutput, calls=%fused_computation.30 | convolution fusion | flops 546308096 | bytes 7340032 | tf_op jit(solution)/shard_map/dot_general | solution.py:723
  14.1 0.7 convolution_convert_fusion.h_ref
  15.5 8.8 %shard_map.102 = (bf16[64,112,128]{2,1,0:T(8,128)(2,1)S(1)}, s32[64,1,128]{2,1,0:T(1,128)S(1)}) custom-call(s32[1,1152]{1,0:T(1,128)S(1)} %broadcast_in_dim.133.slot_ref, bf16[1152,256]{1,0:T(8,128)(2,1)S(1)} %fusion.17.vals_ref), custom_call_target="tpu_custom_call" | custom-call | tf_op jit(solution)/shard_map/pallas_call | solution.py:96
  24.4 1.3 copy-done.4
  25.6 1.2 broadcast_select_fusion.2.want_ref
  26.9 47.2 %shard_map.103 = (bf16[64,112,128]{2,1,0:T(8,128)(2,1)}, s32[8,128]{1,0:T(8,128)}) custom-call(s32[64,1,128]{2,1,0:T(1,128)} %broadcast_select_fusion.2.want_ref, bf16[16384,128]{1,0:T(8,128)(2,1)} %tab_ref.1), custom_call_target="tpu_custom_call" | custom-call | tf_op jit(solution)/shard_map/pallas_call | solution.py:208
  74.1 4.2 %gather_fusion.1 = bf16[1088,128]{1,0:T(8,128)(2,1)S(1)} fusion(bf16[7168,128]{1,0:T(8,128)(2,1)} %bitcast.125, s32[2048]{0:T(1024)S(1)} %pad_clamp_fusion.1), kind=kCustom, calls=%fused_computation.1 | custom fusion | bytes 561408 | tf_op jit(solution)/shard_map/jit(_take)/gather | solution.py:742
  78.3 27.2 %shard_map.104 = (bf16[128,64,128]{2,1,0:T(8,128)(2,1)}, s32[8,128]{1,0:T(8,128)}) custom-call(bf16[1088,128]{1,0:T(8,128)(2,1)S(1)} %gather_fusion.1, s32[8,128]{1,0:T(8,128)} %get-tuple-element.258.most_ref), custom_call_target="tpu_custom_call" | custom-call | tf_op jit(solution)/shard_map/pallas_call | solution.py:265
  105.5 1.3 slice.73
  106.8 0.8 while.24
  107.6 38.0 %shard_map.105 = (f32[8192,128]{1,0:T(8,128)}, bf16[1024,128]{1,0:T(8,128)(2,1)}, f32[1024,128]{1,0:T(8,128)S(1)}, f32[8,128]{1,0:T(8,128)}) custom-call(bf16[8192,128]{1,0:T(8,128)(2,1)} %bitcast.126, bf16[1024,128]{1,0:T(8,128)(2,1)} %copy-done.7, bf16[1088,128]{1,0:T(8,128)(2,1)S(1)} %get-tuple-element.262.t_ref, s32[1024,128]{1,0:T(8,128)} %broadcast_in_dim.134.y_ref, ...), custom_call_target="tpu_custom_call" | custom-call | tf_op jit(solution)/shard_map/pallas_call | solution.py:363
  145.6 6.6 %fusion.12 = f32[256,1024]{0,1:T(8,128)} fusion(bf16[1024,256]{1,0:T(8,128)(2,1)S(1)} %copy-done, f32[1024,1024]{1,0:T(8,128)} %get-tuple-element.380, bf16[1024,128]{1,0:T(8,128)(2,1)} %get-tuple-element.264, bf16[1024,128]{1,0:T(8,128)(2,1)S(1)} %copy-done.8), kind=kOutput, calls=%fused_computation.34 | convolution fusion | flops 826277888 | bytes 6291456 | tf_op jit(solution)/shard_map/ti,tf->if/dot_general | solution.py:767
  152.2 2.3 fusion.42
  154.5 1.6 copy.60
  156.6 1.2 pad_maximum_fusion.rest_ref
  157.8 1.2 slice.78
  159.0 10.8 %shard_map.106 = (f32[4,4,4,32,128]{4,3,2,1,0:T(8,128)}, f32[4,4,4,32,128]{4,3,2,1,0:T(8,128)}, f32[4,4,4,24,128]{4,3,2,1,0:T(8,128)}) custom-call(f32[2,64,2,32,128]{4,3,2,1,0:T(8,128)} %bitcast.113, f32[2,64,24,128]{3,2,1,0:T(8,128)} %pad_maximum_fusion.rest_ref), custom_call_target="tpu_custom_call" | custom-call | tf_op jit(solution)/shard_map/pallas_call | solution.py:428
  171.1 5.2 %shard_map.107.refs_4_ = f32[64,8,128]{2,1,0:T(8,128)S(1)} custom-call(f32[64,8,128]{2,1,0:T(8,128)S(1)} %stack.74.base_ref, s32[1024,128]{1,0:T(8,128)S(1)} %broadcast_in_dim.141.slot_ref, f32[1024,128]{1,0:T(8,128)S(1)} %get-tuple-element.596.dz_ref), custom_call_target="tpu_custom_call" | custom-call | tf_op jit(solution)/shard_map/pallas_call | solution.py:132
  177.0 82.2 %shard_map.108 = (f32[4,4,4,32,128]{4,3,2,1,0:T(8,128)}, f32[4,4,4,32,128]{4,3,2,1,0:T(8,128)}, f32[4,4,4,24,128]{4,3,2,1,0:T(8,128)}, bf16[64,112,128]{2,1,0:T(8,128)(2,1)}, f32[64,8,128]{2,1,0:T(8,128)}) custom-call(f32[4,4,4,32,128]{4,3,2,1,0:T(8,128)} %get-tuple-element.265.refs_0_, f32[4,4,4,32,128]{4,3,2,1,0:T(8,128)} %get-tuple-element.266.refs_1_, ...), custom_call_target="tpu_custom_call" | custom-call | tf_op jit(solution)/shard_map/pallas_call | solution.py:537
  259.2 15.4 %shard_map.109 = (f32[2,2,4,4,4,32,128]{6,5,4,3,2,1,0:T(8,128)}, f32[1,2,4,4,4,24,128]{6,5,4,3,2,1,0:T(8,128)}, bf16[1,2,64,112,128]{4,3,2,1,0:T(8,128)(2,1)}, f32[1,2,64,8,128]{4,3,2,1,0:T(8,128)}) custom-call(f32[4,4,4,32,128]{4,3,2,1,0:T(8,128)} %get-tuple-element.271.refs_0_, f32[4,4,4,32,128]{4,3,2,1,0:T(8,128)} %get-tuple-element.272.refs_1_, ...), custom_call_target="tpu_custom_call" | custom-call | tf_op jit(solution)/shard_map/pallas_call | solution.py:569
  274.6 1.1 copy.64
  277.1 0.8 fusion.21
  279.1 44.2 %shard_map.110 = f32[16384,128]{1,0:T(8,128)} custom-call(s32[128,112]{1,0:T(8,128)} %get-tuple-element.370.refs_0_, s32[128]{0:T(128)} %get-tuple-element.310.refs_1_, bf16[14336,128]{1,0:T(8,128)(2,1)} %bitcast.120, f32[128,112]{1,0:T(8,128)} %get-tuple-element.369.refs_3_, s32[128,64]{1,0:T(8,128)} %get-tuple-element.368.refs_4_, ...), custom_call_target="tpu_custom_call" | custom-call | tf_op jit(solution)/shard_map/pallas_call | solution.py:666
  323.3 0.9 while.25
  324.2 1.7 copy.65
  325.9 0.8 slice_bitcast_fusion.1
  327.1 1.2 copy.71
  (60 shorter events, 9.7 us)
Async XLA Ops:
  0.6 9.0 %copy-start = (bf16[1024,256]{1,0:T(8,128)(2,1)S(1)}, bf16[1024,256]{1,0:T(8,128)(2,1)}, u32[]{:S(2)}) copy-start(bf16[1024,256]{1,0:T(8,128)(2,1)} %param.11) | copy-start | bytes 1572868
  9.6 4.5 %copy-start.8 = (bf16[1024,128]{1,0:T(8,128)(2,1)S(1)}, bf16[1024,128]{1,0:T(8,128)(2,1)}, u32[]{:S(2)}) copy-start(bf16[1024,128]{1,0:T(8,128)(2,1)} %param.13) | copy-start | bytes 786436
  14.1 1.3 copy-start.6
  15.4 62.9 %copy-start.7 = (bf16[1024,128]{1,0:T(8,128)(2,1)}, bf16[1024,128]{1,0:T(8,128)(2,1)S(1)}, u32[]{:S(2)}) copy-start(bf16[1024,128]{1,0:T(8,128)(2,1)S(1)} %convolution_convert_fusion.h_ref) | copy-start | bytes 786436
  24.4 1.3 copy-start.4
  145.6 6.6 %copy-start.9 = (bf16[1024,128]{1,0:T(8,128)(2,1)S(1)}, bf16[1024,128]{1,0:T(8,128)(2,1)}, u32[]{:S(2)}) copy-start(bf16[1024,128]{1,0:T(8,128)(2,1)} %get-tuple-element.264) | copy-start | bytes 786436
  176.3 0.7 copy-start.5
  324.2 4.1 %copy-start.1 = (bf16[1024,256]{1,0:T(8,128)(2,1)S(1)}, bf16[1024,256]{1,0:T(8,128)(2,1)}, u32[]{:S(2)}) copy-start(bf16[1024,256]{1,0:T(8,128)(2,1)} %param.11) | copy-start | bytes 1572868
